TPU v7x, 128 devices: a whole 4x4x4 slice. The times are simulated.
128 devices in a mesh: front: 8 (over y_hi, z), tile: 16 (over x, y_lo, core).
Axes of the slice: x: 4, y: 4 (y_hi: 2, y_lo: 2; y = y_hi * 2 + y_lo), z: 4, core: 2. Of those that a mesh axis runs over, the one named last changes fastest.
Arguments:
- lower_basis: bfloat16 [8, 16, 512, 1024], P('front', 'tile'), may hold values from -0.75 to 0.75
- lower_coeff: bfloat16 [8, 16, 512, 1024], P('front', 'tile'), may hold values from -0.75 to 0.75
- upper_basis: bfloat16 [8, 16, 512, 1024], P('front', 'tile'), may hold values from -0.75 to 0.75
- upper_coeff: bfloat16 [8, 16, 512, 1024], P('front', 'tile'), may hold values from -0.75 to 0.75
- lower_rank: int32 [8, 16, 32], P('front', 'tile'), may hold values from 1 to 32
- upper_rank: int32 [8, 16, 32], P('front', 'tile'), may hold values from 1 to 32
- child_half: int32 [8, 16], replicated, may hold values from 0 to 1
- owner_shift: int32 [2, 32], replicated, may hold values from 0 to 3
Outputs:
- parent_tiles: bfloat16 [8, 16, 8192, 512], P('front', 'tile')
Inputs may be any that keep to these rules, and one draw needn't show every extreme that they name: `child_half`: 0 keeps a tile's index, 1 moves it by 16.
All inputs are finite; a program needn't handle non-finite values.
Results may differ from a plain program's by a relative error of at most 0.0062.
Values may be sent and summed in bfloat16 or wider, within the bound.
A program may use at most 192 MiB of HBM per device.

v0:
```python
import jax
import jax.numpy as jnp
from jax import lax
from jax.sharding import PartitionSpec as P

B = 512
R = 32
KP = 32


def partner(block, axis, apart):
    count = lax.axis_size(axis)
    route = []
    for low in range(count):
        high = low | 1 << apart
        if high != low and high < count:
            route += [(low, high), (high, low)]
    return lax.ppermute(block, axis, route)


def keep_columns(ranks):
    return (jnp.arange(R, dtype=jnp.int32)[None, :] < ranks[:, None]).reshape(KP * R)


def per_device(
    lower_basis,
    lower_coeff,
    upper_basis,
    upper_coeff,
    lower_rank,
    upper_rank,
    child_half,
    owner_shift,
):
    tile_count = lax.axis_size("tile")
    quarter = tile_count // 4
    zero_value = jnp.zeros((), jnp.bfloat16)
    lower_local = jnp.where(keep_columns(lower_rank[0, 0])[None, :], lower_basis[0, 0], zero_value)
    upper_kept = jnp.where(keep_columns(upper_rank[0, 0])[None, :], upper_coeff[0, 0], zero_value)
    upper_local = upper_basis[0, 0].reshape(B, KP, R)
    row_bases = lax.all_gather(lower_local[None], "tile", axis=0, tiled=True)
    coeffs = lax.all_gather(lower_coeff[0], "tile", axis=0, tiled=True)
    piece_rows = row_bases.shape[0]
    middle = jnp.einsum(
        "nbkr,bks->nkrs",
        coeffs.reshape(piece_rows, B, KP, R),
        upper_local,
        preferred_element_type=jnp.float32,
    ).astype(jnp.bfloat16)
    widened = jnp.einsum(
        "nbkr,nkrs->nbks",
        row_bases.reshape(piece_rows, B, KP, R),
        middle,
        preferred_element_type=jnp.float32,
    ).astype(jnp.bfloat16)
    widened = widened.reshape(piece_rows, B, KP * R)
    tiles = jnp.einsum(
        "nbk,ck->nbc", widened, upper_kept, preferred_element_type=jnp.float32
    ).astype(jnp.bfloat16)
    front_idx = lax.axis_index("front")
    tile_idx = lax.axis_index("tile")
    parent = front_idx // 4
    my_child = front_idx % 4
    shifts = lax.dynamic_index_in_dim(owner_shift, parent, 0, keepdims=False)
    own_halves = lax.dynamic_index_in_dim(child_half, front_idx, 0, keepdims=False)
    own_col_half = lax.dynamic_index_in_dim(own_halves, tile_idx, 0, keepdims=False)
    col_shift = lax.dynamic_index_in_dim(
        shifts, tile_idx + tile_count * own_col_half, 0, keepdims=False
    )
    outgoing_all = jnp.roll(tiles.reshape(quarter, 4, B, B), col_shift, axis=1)
    partner_high = my_child ^ 2
    outgoing = lax.dynamic_slice_in_dim(outgoing_all, 2 * (partner_high // 2), 2, 1)
    kept = lax.dynamic_slice_in_dim(outgoing_all, 2 * (my_child // 2), 2, 1)
    received = partner(outgoing, "front", 1)
    holding = jnp.stack([kept, received], axis=1)
    leaving = lax.dynamic_index_in_dim(holding, (my_child ^ 1) % 2, 2, keepdims=False)
    staying = lax.dynamic_index_in_dim(holding, my_child % 2, 2, keepdims=False)
    incoming = partner(leaving, "front", 0)
    blocks = jnp.concatenate([staying, incoming], axis=1)
    sources = my_child ^ jnp.array([0, 2, 1, 3], dtype=jnp.int32)
    slot_range = jnp.arange(tile_count, dtype=jnp.int32)
    group_range = jnp.arange(quarter, dtype=jnp.int32)
    assembled = jnp.zeros((tile_count, B * B), jnp.float32)
    for source in range(4):
        child_front = 4 * parent + sources[source]
        halves = lax.dynamic_index_in_dim(child_half, child_front, 0, keepdims=False)
        col_half = lax.dynamic_index_in_dim(halves, tile_idx, 0, keepdims=False)
        child_shift = lax.dynamic_index_in_dim(
            shifts, tile_idx + tile_count * col_half, 0, keepdims=False
        )
        residue = (my_child - child_shift) % 4
        row_halves = lax.dynamic_index_in_dim(
            halves.reshape(quarter, 4), residue, 1, keepdims=False
        )
        slot_ids = col_half * (tile_count // 2) + group_range + quarter * row_halves
        one_hot = (slot_ids[None, :] == slot_range[:, None]).astype(jnp.bfloat16)
        one_block = blocks[:, source].reshape(quarter, B * B)
        assembled = assembled + jnp.dot(one_hot, one_block, preferred_element_type=jnp.float32)
    return assembled.astype(jnp.bfloat16).reshape(1, 1, tile_count * B, B)


def solution(mesh):
    in_specs = (
        P("front", "tile", None, None),
        P("front", "tile", None, None),
        P("front", "tile", None, None),
        P("front", "tile", None, None),
        P("front", "tile", None),
        P("front", "tile", None),
        P(),
        P(),
    )
    out_specs = P("front", "tile", None, None)
    return jax.shard_map(
        per_device, mesh=mesh, in_specs=in_specs, out_specs=out_specs, check_vma=False
    )
```

profile of v0, /device:TPU:1, one launch (start us, length us, event | category | flops | bytes accessed | tf_op | source)
XLA Modules:
  0.0 498.2 jit_solution(14620249598489331912)
XLA Ops:
  8.1 2.3 bitcast_select_fusion
  20.9 83.4 %all-gather.6.cloned.1.call-done = bf16[16,1,512,1024]{3,2,1,0:T(8,128)(2,1)} async-done(((bf16[1,1,512,1024]{3,2,1,0:T(8,128)(2,1)}), bf16[16,1,512,1024]{3,2,1,0:T(8,128)(2,1)}) %all-gather.6.cloned.1.call-update) | async-done | bytes 16777232 | tf_op jit(solution)/shard_map/all_gather | solution.py:42
  104.3 22.0 %copy.17 = bf16[16,1,512,1024]{2,3,0,1:T(8,128)(2,1)} copy(bf16[16,1,512,1024]{3,2,1,0:T(8,128)(2,1)} %all-gather.6.cloned.1.call-done) | data formatting | bytes 33554432 | tf_op jit(solution)/shard_map/all_gather | solution.py:42
  126.2 72.0 %all-gather.4.cloned.1.call-done = bf16[16,512,1024]{2,1,0:T(8,128)(2,1)} async-done(((bf16[1,512,1024]{2,1,0:T(8,128)(2,1)}), bf16[16,512,1024]{2,1,0:T(8,128)(2,1)}) %all-gather.4.cloned.1.call-update) | async-done | bytes 16777232 | tf_op jit(solution)/shard_map/all_gather | solution.py:41
  198.3 21.6 %copy.18 = bf16[16,512,1024]{1,2,0:T(8,128)(2,1)} copy(bf16[16,512,1024]{2,1,0:T(8,128)(2,1)} %all-gather.4.cloned.1.call-done) | data formatting | bytes 33554432 | tf_op jit(solution)/shard_map/all_gather | solution.py:41
  219.9 23.9 %convolution_convert_fusion = bf16[16,32,32,512]{3,2,1,0:T(8,128)(2,1)} fusion(bf16[16,512,32,32]{1,3,2,0:T(8,128)(2,1)} %bitcast.75, bf16[512,32,32,1]{0,2,1,3:T(8,128)(2,1)S(1)} %bitcast.77, bf16[16,512,32,32]{1,3,2,0:T(8,128)(2,1)} %bitcast.74), kind=kOutput, calls=%fused_computation.8 | convolution fusion | flops 1082654720 | bytes 51380224 | tf_op jit(solution)/shard_map/nbkr,nkrs->nbks/dot_general | solution.py:50
  243.8 12.6 %convolution_convert_fusion.1 = bf16[16,512,512]{2,1,0:T(8,128)(2,1)S(1)} fusion(bf16[16,512,1024]{1,2,0:T(8,128)(2,1)} %bitcast.76, bf16[1,1,512,1024]{3,2,1,0:T(8,128)(2,1)S(1)} %copy-done.4, pred[1024]{0:T(1024)(128)(4,1)S(1)} %lt.170), kind=kOutput, calls=%fused_computation.13 | convolution fusion | flops 8594653184 | bytes 26215424 | tf_op jit(solution)/shard_map/nbk,ck->nbc/dot_general | solution.py:57
  256.4 5.0 %fusion.5 = (bf16[4,2,512,512]{3,2,1,0:T(8,128)(2,1)}, bf16[4,1,2,512,512]{4,3,2,0,1:T(8,128)(2,1)}) fusion(s32[]{:T(128)S(6)} %dynamic_slice.90, bf16[4,4,512,512]{3,2,1,0:T(8,128)(2,1)S(1)} %bitcast.82, s32[]{:T(128)S(6)} %dynamic_slice.88), kind=kLoop, calls=%fused_computation.18 | loop fusion | flops 4194304 | bytes 16777224 | tf_op jit(solution)/shard_map/jit(_roll_dynamic)/concatenate | solution.py:70
  261.4 2.9 collective-permute-start
  264.3 90.8 %collective-permute-done = bf16[4,2,512,512]{3,2,1,0:T(8,128)(2,1)} collective-permute-done((bf16[4,2,512,512]{3,2,1,0:T(8,128)(2,1)}, bf16[4,2,512,512]{3,2,1,0:T(8,128)(2,1)}, u32[]{:S(2)}, u32[]{:S(2)}) %collective-permute-start) | collective-permute-done | bytes 4194336 | tf_op jit(solution)/shard_map/ppermute | solution.py:18
  355.1 5.9 %fusion.2 = (bf16[4,2,512,512]{3,2,0,1:T(8,128)(2,1)}, bf16[4,2,512,512]{3,2,0,1:T(8,128)(2,1)}) fusion(s32[]{:T(128)S(6)} %select_n.213, bf16[4,1,2,512,512]{4,3,2,0,1:T(8,128)(2,1)} %get-tuple-element.12, bf16[4,1,2,512,512]{4,3,2,0,1:T(8,128)(2,1)} %bitcast.20, s32[]{:T(128)S(6)} %select_n.199), kind=kLoop, calls=%fused_computation.15 | loop fusion | flops 4194304 | bytes 16777224 | tf_op jit(solution)/shard_map/jit(dynamic_index_in_dim)/squeeze | solution.py:76
  361.0 1.3 collective-permute-start.1
  368.2 2.5 slice_bitcast_fusion.2
  370.7 1.6 copy.22
  372.3 1.6 copy.21
  374.0 8.0 %fusion.16 = f32[16,262144]{1,0:T(8,128)} fusion(bf16[4,262144]{1,0:T(4,128)(2,1)S(1)} %bitcast.78, s32[4]{0:T(128)S(1)} %add_add_fusion.3), kind=kOutput, calls=%fused_computation.39 | convolution fusion | flops 33554496 | bytes 18874384 | tf_op jit(solution)/shard_map/dot_general | solution.py:98
  382.0 13.8 %convolution_add_fusion.2 = f32[16,262144]{1,0:T(8,128)} fusion(f32[16,262144]{1,0:T(8,128)} %fusion.16, bf16[4,262144]{1,0:T(4,128)(2,1)S(1)} %bitcast.80, s32[4]{0:T(128)S(1)} %add_add_fusion.2), kind=kOutput, calls=%fused_computation.2 | convolution fusion | flops 37748800 | bytes 35651600 | tf_op jit(solution)/shard_map/dot_general | solution.py:98
  395.8 56.6 %collective-permute-done.1 = bf16[4,2,512,512]{3,2,0,1:T(8,128)(2,1)} collective-permute-done((bf16[4,2,512,512]{3,2,0,1:T(8,128)(2,1)}, bf16[4,2,512,512]{3,2,0,1:T(8,128)(2,1)}, u32[]{:S(2)}, u32[]{:S(2)}) %collective-permute-start.1) | collective-permute-done | bytes 4194336 | tf_op jit(solution)/shard_map/ppermute | solution.py:18
  452.3 2.5 slice_bitcast_fusion
  454.8 1.6 copy.24
  456.5 1.8 copy.23
  458.3 13.8 %convolution_add_fusion.1 = f32[16,262144]{1,0:T(8,128)} fusion(f32[16,262144]{1,0:T(8,128)} %convolution_add_fusion.2, bf16[4,262144]{1,0:T(4,128)(2,1)S(1)} %bitcast.81, s32[4]{0:T(128)S(1)} %add_add_fusion.1), kind=kOutput, calls=%fused_computation.1 | convolution fusion | flops 37748800 | bytes 35651600 | tf_op jit(solution)/shard_map/dot_general | solution.py:98
  472.1 11.3 %fusion = bf16[16,262144]{1,0:T(8,128)(2,1)} fusion(f32[16,262144]{1,0:T(8,128)} %convolution_add_fusion.1, bf16[4,262144]{1,0:T(4,128)(2,1)S(1)} %bitcast.79, s32[4]{0:T(128)S(1)} %add_add_fusion), kind=kOutput, calls=%fused_computation.3 | convolution fusion | flops 41943104 | bytes 27262992 | tf_op jit(solution)/shard_map/dot_general | solution.py:98
  483.4 8.0 %reshape.193 = bf16[1,1,8192,512]{3,2,1,0:T(8,128)(2,1)} reshape(bf16[16,262144]{1,0:T(8,128)(2,1)} %fusion) | data formatting | bytes 16777216 | tf_op jit(solution)/shard_map/reshape | solution.py:99
  (36 shorter events, 5.1 us)
Async XLA Ops:
  6.5 4.0 copy-start.5
  6.5 7.2 %copy-start.2 = (s32[8,16]{1,0:T(8,128)S(1)}, s32[8,16]{1,0:T(8,128)}, u32[]{:S(2)}) copy-start(s32[8,16]{1,0:T(8,128)} %param.15) | copy-start | bytes 1540
  6.5 11.1 %copy-start.1 = (s32[2,32]{1,0:T(2,128)S(1)}, s32[2,32]{1,0:T(2,128)}, u32[]{:S(2)}) copy-start(s32[2,32]{1,0:T(2,128)} %param.16) | copy-start | bytes 772
  6.5 13.7 %copy-start.3 = (s32[1,1,32]{2,1,0:T(1,128)S(1)}, s32[1,1,32]{2,1,0:T(1,128)}, u32[]{:S(2)}) copy-start(s32[1,1,32]{2,1,0:T(1,128)} %param.14) | copy-start | bytes 388
  6.5 13.8 %copy-start = (bf16[1,1,512,1024]{3,2,1,0:T(8,128)(2,1)S(1)}, bf16[1,1,512,1024]{3,2,1,0:T(8,128)(2,1)}, u32[]{:S(2)}) copy-start(bf16[1,1,512,1024]{3,2,1,0:T(8,128)(2,1)} %param.11) | copy-start | bytes 3145732
  6.5 97.7 %all-gather.6.cloned.1.call-start = ((), (), s32[]{:S(2)}) async-start(), calls=%async_computation.1 | async-start | bytes 17825792 | tf_op jit(solution)/shard_map/all_gather | solution.py:42
  7.3 191.0 %all-gather.4.cloned.1.call-start = ((), (), s32[]{:S(2)}) async-start(), calls=%async_computation | async-start | bytes 17825792 | tf_op jit(solution)/shard_map/all_gather | solution.py:41
  219.9 23.9 %copy-start.4 = (bf16[1,1,512,1024]{3,2,1,0:T(8,128)(2,1)S(1)}, bf16[1,1,512,1024]{3,2,1,0:T(8,128)(2,1)}, u32[]{:S(2)}) copy-start(bf16[1,1,512,1024]{3,2,1,0:T(8,128)(2,1)} %param.12) | copy-start | bytes 3145732
  261.4 93.7 %collective-permute-start = (bf16[4,2,512,512]{3,2,1,0:T(8,128)(2,1)}, bf16[4,2,512,512]{3,2,1,0:T(8,128)(2,1)}, u32[]{:S(2)}, u32[]{:S(2)}) collective-permute-start(bf16[4,2,512,512]{3,2,1,0:T(8,128)(2,1)} %get-tuple-element.11), channel_id=1, source_target_pairs={{0,32},{32,0},{16,48},{48,16},{64,96},{96,64},{80,112},{112,80},{1... | collective-permute-start | bytes 12582920 | tf_op jit(solution)/shard_map/ppermute | solution.py:18
  361.0 91.3 %collective-permute-start.1 = (bf16[4,2,512,512]{3,2,0,1:T(8,128)(2,1)}, bf16[4,2,512,512]{3,2,0,1:T(8,128)(2,1)}, u32[]{:S(2)}, u32[]{:S(2)}) collective-permute-start(bf16[4,2,512,512]{3,2,0,1:T(8,128)(2,1)} %get-tuple-element.9), channel_id=1, source_target_pairs={{0,16},{16,0},{32,48},{48,32},{64,80},{80,64},{96,112},{112,96},{1... | collective-permute-start | bytes 12582920 | tf_op jit(solution)/shard_map/ppermute | solution.py:18
Sparse Core Ops, SparseCore 0:
  9.1 95.1 all-gather.5
  106.0 92.2 all-gather.3
where the time goes:
time: 500 us; the launch traced here: 498 us
  waiting for transfers between devices  303 us (61%)
  matrix products  83.4 us (17%)
  local copies, waits for them, and re-layouts  66.3 us (13%)
  between operations  26.3 us (5%)
  other arithmetic  14.5 us (3%)
    ppermute x2, waiting for transfers between devices, partner(): return lax.ppermute(block, axis, route)  147 us
    all_gather x1, waiting for transfers between devices, per_device(): coeffs = lax.all_gather(lower_coeff[0], 'tile', axis=0, tiled=True)  83.4 us
    all_gather x1, waiting for transfers between devices, per_device(): row_bases = lax.all_gather(lower_local[None], 'tile', axis=0, tiled=True)  72 us
    dot_general x4, matrix products, per_device(): jnp.dot(one_hot, one_block, preferred_element_type=jnp.float32)  46.9 us
    dot_general x1, matrix products, per_device(): jnp.einsum('nbkr,nkrs->nbks', row_bases.reshape(piece_rows, B, KP, R), mi...  23.9 us
    all_gather x1, local copies, waits for them, and re-layouts, per_device(): coeffs = lax.all_gather(lower_coeff[0], 'tile', axis=0, tiled=True)  22 us
    all_gather x1, local copies, waits for them, and re-layouts, per_device(): row_bases = lax.all_gather(lower_local[None], 'tile', axis=0, tiled=True)  21.6 us
    dot_general x1, matrix products, per_device(): jnp.einsum('nbk,ck->nbc', widened, upper_kept, preferred_element_type=jnp...  12.6 us
  transfers between devices with their start and end apart: 4, of which 4 were waited for; matrix products, arithmetic and copies ran while one was open for 11% of the time, Pallas kernels for 0%

commit v1 on v0

v1 whole, which is shorter than its diff:
```python
import functools

import jax
import jax.numpy as jnp
from jax import lax
from jax.experimental import pallas as pl
from jax.experimental.pallas import tpu as pltpu
from jax.sharding import PartitionSpec as P

MESH = pl.DeviceIdType.MESH
B = 512
R = 32
KP = 32
K = 1024
CH = 4
PR = B // CH
HR = PR // 2
BF = jnp.bfloat16

Y_OPS = (
    [("Y", 0, 0, k) for k in range(CH)]
    + [("X", 0, 0, k) for k in range(CH)]
    + [("X", d, 0, k) for k in range(CH) for d in (1, -1)]
    + [("X", 2, 0, 1), ("X", 2, 0, 3)]
)


def x_ops(sign):
    first = (0, 1) if sign > 0 else (2, 3)
    return (
        [("Y", 0, 0, k) for k in range(CH)]
        + [("Y", 0, 1, k) for k in range(CH)]
        + [("X", 0, 0, k) for k in range(CH)]
        + [("Y", -sign, 0, k) for k in first]
        + [("Y", -sign, 1, k) for k in first]
        + [("X", -sign, 0, k) for k in first[::-1]]
        + [("X", -sign, 1, first[0])]
    )


LINK_OPS = [("y",) + op for op in Y_OPS] + [("+",) + op for op in x_ops(1)] + [("-",) + op for op in x_ops(-1)]
LINK_ID = {op: i for i, op in enumerate(LINK_OPS)}
CORE_OPS = [(kind, dx, dy, k) for kind in "YX" for dx in (0, 1, -1, 2) for dy in (0, 1) for k in range(CH)]
CORE_ID = {op: i for i, op in enumerate(CORE_OPS)}
Z_STEPS = (
    [(0, k) for k in range(CH)]
    + [(d, k) for k in range(CH) for d in (1, -1)]
    + [(2, k) for k in (1, 3, 0, 2)]
)
V_SLOT = {0: 0, 1: 1, -1: 2, 2: 0}


def main_kernel(
    lrank, urank, halves, shifts, xin, yin, pin, qin, out,
    xbuf, ybuf, vbuf, pbuf, ptbuf, qbuf, stage, sbuf, relay,
    in_sem, ls, lr, cs, cr, zs, zr, os_sem,
):
    front, tile = lax.axis_index("front"), lax.axis_index("tile")
    yh, z = front // 4, front % 4
    x, yl, core = tile // 4, (tile // 2) % 2, tile % 2

    def tile_at(gx, gy, gc):
        return (gx * 2 + gy) * 2 + gc

    dev = {
        "y": (front, tile_at(x, 1 - yl, core)),
        "+": (front, tile_at((x + 1) % 4, yl, core)),
        "-": (front, tile_at((x + 3) % 4, yl, core)),
        "c": (front, tile_at(x, yl, 1 - core)),
        "z+": (yh * 4 + (z + 1) % 4, tile),
        "z-": (yh * 4 + (z + 3) % 4, tile),
    }

    def row_of(dx, dy, gc):
        gy = yl if dy == 0 else 1 - yl
        return tile_at((x + dx + 4) % 4, gy, gc)

    bufs = {"X": xbuf, "Y": ybuf}

    def piece(kind, dx, dy, gc, k):
        return bufs[kind].at[row_of(dx, dy, gc), pl.ds(k * PR, PR), :]

    sends = []

    def link_copy(op):
        link, kind, dx, dy, k = op
        ref = piece(kind, dx, dy, core, k)
        i = LINK_ID[op]
        return pltpu.make_async_remote_copy(
            src_ref=ref, dst_ref=ref, send_sem=ls.at[i], recv_sem=lr.at[i],
            device_id=dev[link], device_id_type=MESH,
        )

    def send(link, kind, dx, dy, k):
        copy = link_copy((link, kind, dx, dy, k))
        copy.start()
        sends.append(copy)

    def core_send(kind, dx, dy, k):
        i = CORE_ID[(kind, dx, dy, k)]
        ref = piece(kind, dx, dy, core, k)
        copy = pltpu.make_async_remote_copy(
            src_ref=ref, dst_ref=ref, send_sem=cs.at[i], recv_sem=cr.at[i],
            device_id=dev["c"], device_id_type=MESH,
        )
        copy.start()
        sends.append(copy)

    def core_recv(kind, dx, dy, k):
        i = CORE_ID[(kind, dx, dy, k)]
        ref = piece(kind, dx, dy, 1 - core, k)
        pltpu.make_async_remote_copy(
            src_ref=ref, dst_ref=ref, send_sem=cs.at[i], recv_sem=cr.at[i],
            device_id=dev["c"], device_id_type=MESH,
        ).wait_recv()

    def recv(link, kind, dx, dy, k):
        if link == "y":
            sender = (kind, dx, 1 - dy, k)
        elif link == "+":
            sender = (kind, (dx + 1 + 1) % 4 - 1, dy, k)
        else:
            sender = (kind, (dx - 1 + 1) % 4 - 1, dy, k)
        i = LINK_ID[(link,) + sender]
        ref = piece(kind, dx, dy, core, k)
        pltpu.make_async_remote_copy(
            src_ref=ref, dst_ref=ref, send_sem=ls.at[i], recv_sem=lr.at[i],
            device_id=dev[link], device_id_type=MESH,
        ).wait_recv()
        core_send(kind, dx, dy, k)

    me = tile
    y_loads = []
    for k in range(CH):
        rows = pl.ds(k * PR, PR)
        copy = pltpu.make_async_copy(yin.at[rows, :], ybuf.at[me, rows, :], in_sem.at[k])
        copy.start()
        y_loads.append(copy)
    x_load = pltpu.make_async_copy(xin, xbuf.at[me], in_sem.at[CH])
    p_load = pltpu.make_async_copy(pin, pbuf, in_sem.at[CH + 1])
    q_load = pltpu.make_async_copy(qin, qbuf, in_sem.at[CH + 2])
    x_load.start()
    p_load.start()
    q_load.start()

    barrier = pltpu.get_barrier_semaphore()
    for name in ("y", "+", "-", "c", "z+", "z-"):
        pl.semaphore_signal(barrier, inc=1, device_id=dev[name], device_id_type=MESH)

    col = lax.broadcasted_iota(jnp.int32, (8, K), 1)

    def keep(ranks):
        limit = jnp.zeros((8, K), jnp.int32)
        for k in range(KP):
            limit = jnp.where(col // R == k, ranks[k], limit)
        return (col % R < limit).astype(jnp.float32)

    lkeep = keep(lrank)[:1]
    ukeep = keep(urank)[:1]
    pl.semaphore_wait(barrier, 6)

    def mask_y(k):
        y_loads[k].wait()
        rows = pl.ds(k * PR, PR)
        ybuf[me, rows, :] = (ybuf[me, rows, :].astype(jnp.float32) * lkeep).astype(BF)

    def send_own_y(k):
        for link in ("y", "+", "-"):
            send(link, "Y", 0, 0, k)
        core_send("Y", 0, 0, k)

    mask_y(0)
    for k in range(1, CH):
        mask_y(k)
        send_own_y(k - 1)
    x_load.wait()
    send_own_y(CH - 1)
    for k in range(CH):
        send("y", "X", 0, 0, k)
        core_send("X", 0, 0, k)

    p_load.wait()
    for q in range(4):
        cols = slice(q * 256, (q + 1) * 256)
        part = pbuf[:, cols].astype(jnp.float32) * ukeep[:, cols]
        ptbuf[cols, :] = part.T.astype(BF)
    q_load.wait()

    def same_panel():
        a = lax.broadcasted_iota(jnp.int32, (256, 256), 0) // R
        b = lax.broadcasted_iota(jnp.int32, (256, 256), 1) // R
        return a == b

    def make_v(dx, dy, classes=(0, 1)):
        slot = V_SLOT[dx]
        gy = yl if dy == 0 else 1 - yl

        def body(n, carry):
            gc = (core + classes[0] + n // 4) % 2
            q = n % 4
            cols = pl.ds(pl.multiple_of(q * 256, 256), 256)
            row = tile_at((x + dx + 4) % 4, gy, gc)
            mt = jnp.dot(ptbuf[cols, :], ybuf[row, :, cols], preferred_element_type=jnp.float32)
            mt = jnp.where(same_panel(), mt, 0.0).astype(BF)
            v = jnp.dot(qbuf[:, cols], mt, preferred_element_type=jnp.float32)
            vbuf[slot, gy * 2 + gc, :, cols] = v.astype(BF)
            return carry

        lax.fori_loop(0, 4 * len(classes), body, 0)

    half = halves[front, tile]
    shift = shifts[yh, tile + 16 * half]
    z_copies = []
    own_copies = []

    def z_copy(n, what, src, dst, to):
        return pltpu.make_async_remote_copy(
            src_ref=src, dst_ref=dst, send_sem=zs.at[n, what], recv_sem=zr.at[n, what],
            device_id=dev[to], device_id_type=MESH,
        )

    def z_refs(n, what, receiving=False):
        dx, k = Z_STEPS[n]
        g = (x + dx + 4) % 4
        back = (z + 3) % 4 if receiving else z
        ahead = (z + 1) % 4 if receiving else z
        if what == 0:
            return sbuf.at[n, 2, pl.ds(0, HR), :], relay.at[n, 0], "z+"
        if what == 1:
            return sbuf.at[n, 2, pl.ds(HR, HR), :], relay.at[n, 1], "z-"
        if what == 2:
            return sbuf.at[n, 1], out.at[back, g, pl.ds(k * PR, PR), :], "z+"
        if what == 3:
            return sbuf.at[n, 3], out.at[ahead, g, pl.ds(k * PR, PR), :], "z-"
        if what == 4:
            child = (z + 2) % 4 if receiving else (z + 3) % 4
            return relay.at[n, 0], out.at[child, g, pl.ds(k * PR, HR), :], "z+"
        child = (z + 2) % 4 if receiving else (z + 1) % 4
        return relay.at[n, 1], out.at[child, g, pl.ds(k * PR + HR, HR), :], "z-"

    def z_send(n, what):
        src, dst, to = z_refs(n, what)
        copy = z_copy(n, what, src, dst, to)
        copy.start()
        sends.append(copy)

    def z_wait(n, what):
        src, dst, to = z_refs(n, what, receiving=True)
        z_copy(n, what, src, dst, to).wait_recv()

    def hand_on(n):
        for what in (0, 1):
            z_wait(n, what)
            z_send(n, what + 4)

    def z_step(n):
        dx, k = Z_STEPS[n]
        slot = V_SLOT[dx]
        g = (x + dx + 4) % 4

        def body(r, carry):
            acc = lax.dot_general(
                xbuf[g * 4 + r, pl.ds(k * PR, PR), :],
                vbuf[slot, r],
                (((1,), (1,)), ((), ())),
                preferred_element_type=jnp.float32,
            )
            stage[r] = acc.astype(BF)
            return carry

        lax.fori_loop(0, 4, body, 0)
        for rel in (2, 1, 3, 0):
            sbuf[n, rel] = stage[(z + rel - shift + 4) % 4]
        for what in (0, 1, 2, 3):
            z_send(n, what)
        copy = pltpu.make_async_copy(sbuf.at[n, 0], out.at[z, g, pl.ds(k * PR, PR), :], os_sem.at[n])
        copy.start()
        own_copies.append(copy)
        if n > 0:
            hand_on(n - 1)

    for k in range(CH):
        core_recv("Y", 0, 0, k)
    make_v(0, 0)
    for k in range(CH):
        recv("y", "Y", 0, 1, k)
        send("+", "Y", 0, 1, k)
        send("-", "Y", 0, 1, k)
        recv("+", "Y", -1, 0, k)
        recv("-", "Y", 1, 0, k)
    for k in range(CH):
        send("+", "X", 0, 0, k)
        send("-", "X", 0, 0, k)
    for k in range(CH):
        core_recv("Y", 0, 1, k)
    make_v(0, 1)
    for k in range(CH):
        recv("y", "X", 0, 1, k)
        recv("+", "Y", -1, 1, k)
        recv("-", "Y", 1, 1, k)
        core_recv("X", 0, 0, k)
        core_recv("X", 0, 1, k)
        z_step(k)
        if k in (1, 2):
            d = 1 if k == 1 else -1
            for j in range(CH):
                core_recv("Y", d, 0, j)
            make_v(d, 0)
    for d in (1, -1):
        for k in range(CH):
            core_recv("Y", d, 1, k)
        make_v(d, 1)
    for k in range(CH):
        recv("-", "X", 1, 0, k)
        send("y", "X", 1, 0, k)
        recv("+", "X", -1, 0, k)
        send("y", "X", -1, 0, k)
        if k == 0:
            for j in (0, 1):
                send("+", "Y", -1, 0, j)
                send("-", "Y", 1, 0, j + 2)
            for j in (0, 1):
                send("+", "Y", -1, 1, j)
                send("-", "Y", 1, 1, j + 2)
        if k == 3:
            for j in (1, 0):
                send("+", "X", -1, 0, j)
                send("-", "X", 1, 0, j + 2)
        if k >= 1:
            n = CH + 2 * (k - 1)
            for d in (1, -1):
                recv("y", "X", d, 1, k - 1)
                core_recv("X", d, 0, k - 1)
                core_recv("X", d, 1, k - 1)
                z_step(n + (d < 0))
    send("+", "X", -1, 1, 0)
    send("-", "X", 1, 1, 2)
    for j in (0, 1):
        recv("+", "Y", 2, 0, j)
        recv("-", "Y", 2, 0, j + 2)
    for d in (1, -1):
        recv("y", "X", d, 1, 3)
        core_recv("X", d, 0, 3)
        core_recv("X", d, 1, 3)
        z_step(CH + 6 + (d < 0))
        if d == 1:
            for j in range(CH):
                core_recv("Y", 2, 0, j)
            make_v(2, 0)
    for j in (0, 1):
        recv("+", "Y", 2, 1, j)
        recv("-", "Y", 2, 1, j + 2)
    for j in range(CH):
        core_recv("Y", 2, 1, j)
    make_v(2, 1)
    recv("+", "X", 2, 0, 1)
    send("y", "X", 2, 0, 1)
    recv("-", "X", 2, 0, 3)
    send("y", "X", 2, 0, 3)
    recv("+", "X", 2, 0, 0)
    recv("-", "X", 2, 0, 2)
    recv("y", "X", 2, 1, 1)
    recv("+", "X", 2, 1, 0)
    recv("-", "X", 2, 1, 2)
    recv("y", "X", 2, 1, 3)
    for n in range(3 * CH, 4 * CH):
        core_recv("X", 2, 0, Z_STEPS[n][1])
        core_recv("X", 2, 1, Z_STEPS[n][1])
        z_step(n)
    hand_on(4 * CH - 1)
    for n in range(4 * CH):
        for what in (2, 3, 4, 5):
            z_wait(n, what)
    for copy in own_copies:
        copy.wait()
    for copy in sends:
        copy.wait_send()


def main_call(xin, yin, pin, qin, lrank, urank, halves, shifts):
    hbm = pl.BlockSpec(memory_space=pl.ANY)
    smem = pl.BlockSpec(memory_space=pltpu.SMEM)
    steps = 4 * CH
    return pl.pallas_call(
        main_kernel,
        out_shape=jax.ShapeDtypeStruct((4, 4, B, B), BF),
        in_specs=[smem] * 4 + [hbm] * 4,
        out_specs=hbm,
        scratch_shapes=[
            pltpu.VMEM((16, B, K), BF),
            pltpu.VMEM((16, B, K), BF),
            pltpu.VMEM((3, 4, B, K), BF),
            pltpu.VMEM((B, K), BF),
            pltpu.VMEM((K, B), BF),
            pltpu.VMEM((B, K), BF),
            pltpu.VMEM((4, PR, B), BF),
            pltpu.VMEM((steps, 4, PR, B), BF),
            pltpu.VMEM((steps, 2, HR, B), BF),
            pltpu.SemaphoreType.DMA((CH + 3,)),
            pltpu.SemaphoreType.DMA((len(LINK_OPS),)),
            pltpu.SemaphoreType.DMA((len(LINK_OPS),)),
            pltpu.SemaphoreType.DMA((len(CORE_OPS),)),
            pltpu.SemaphoreType.DMA((len(CORE_OPS),)),
            pltpu.SemaphoreType.DMA((steps, 6)),
            pltpu.SemaphoreType.DMA((steps, 6)),
            pltpu.SemaphoreType.DMA((steps,)),
        ],
        compiler_params=pltpu.CompilerParams(
            collective_id=0, has_side_effects=True, vmem_limit_bytes=64_000_000
        ),
        name="gather_update_exchange",
    )(lrank, urank, halves, shifts, xin, yin, pin, qin)


def sum_kernel(halves, shifts, blocks, out):
    front, tile = lax.axis_index("front"), lax.axis_index("tile")
    parent, o = front // 4, front % 4
    g = pl.program_id(0)
    place = []
    for c in range(4):
        child = 4 * parent + c
        col_half = halves[child, tile]
        row = 4 * g + (o - shifts[parent, tile + 16 * col_half] + 4) % 4
        place.append(2 * col_half + halves[child, row])
    for s in range(4):
        total = jnp.zeros(blocks.shape[2:], jnp.float32)
        for c in range(4):
            total = total + jnp.where(place[c] == s, blocks[c, 0].astype(jnp.float32), 0.0)
        out[s, 0] = total.astype(BF)


def sum_call(halves, shifts, blocks):
    rows = B // 2
    smem = pl.BlockSpec(memory_space=pltpu.SMEM)
    block = pl.BlockSpec((4, 1, rows, B), lambda g, i: (0, g, i, 0))
    return pl.pallas_call(
        sum_kernel,
        grid=(4, 2),
        out_shape=jax.ShapeDtypeStruct((4, 4, B, B), BF),
        in_specs=[smem, smem, block],
        out_specs=block,
        name="sum_into_slots",
    )(halves, shifts, blocks)


def per_device(lower_basis, lower_coeff, upper_basis, upper_coeff, lower_rank, upper_rank, child_half, owner_shift):
    blocks = main_call(
        lower_basis[0, 0], lower_coeff[0, 0], upper_basis[0, 0], upper_coeff[0, 0],
        lower_rank[0, 0], upper_rank[0, 0], child_half, owner_shift,
    )
    return sum_call(child_half, owner_shift, blocks).reshape(1, 1, 16 * B, B)


def solution(mesh):
    whole = P("front", "tile", None, None)
    ranks = P("front", "tile", None)
    return jax.shard_map(
        per_device,
        mesh=mesh,
        in_specs=(whole, whole, whole, whole, ranks, ranks, P(), P()),
        out_specs=whole,
        check_vma=False,
    )
```

time: 500 us -> 186 us (0.37)
  waiting for transfers between devices: 303 us -> 0 us
  Pallas kernels: 0 us -> 184 us
  matrix products: 83.4 us -> 0 us
  local copies, waits for them, and re-layouts: 66.3 us -> 0 us
  between operations: 26.3 us -> 0.01 us
  other arithmetic: 14.5 us -> 0 us
    pallas_call x0 -> x2, Pallas kernels: none -> 184 us  [the longest x1 173 us: main_call(): pl.pallas_call(main_kernel, out_shape=jax.ShapeDtypeStruct((4, 4, B, B),...]
    all_gather x2 -> x0, waiting for transfers between devices: 155 us -> none  [the longest x1 83.4 us: per_device(): coeffs = lax.all_gather(lower_coeff[0], 'tile', axis=0, tiled=True)]
    ppermute x2 -> x0, waiting for transfers between devices: 147 us -> none  [partner(): return lax.ppermute(block, axis, route)]
    dot_general x6 -> x0, matrix products: 83.4 us -> none  [the longest x4 46.9 us: per_device(): jnp.dot(one_hot, one_block, preferred_element_type=jnp.float32)]
    all_gather x2 -> x0, local copies, waits for them, and re-layouts: 43.6 us -> none  [the longest x1 22 us: per_device(): coeffs = lax.all_gather(lower_coeff[0], 'tile', axis=0, tiled=True)]
    unnamed x19 -> x0, local copies, waits for them, and re-layouts: 12.3 us -> none
    reshape x5 -> x0, local copies, waits for them, and re-layouts: 8.32 us -> none  [the longest x1 8 us: per_device(): return assembled.astype(jnp.bfloat16).reshape(1, 1, tile_count * B, B)]
    squeeze x1 -> x0, other arithmetic: 5.89 us -> none  [per_device(): lax.dynamic_index_in_dim(holding, (my_child ^ 1) % 2, 2, keepdims=False)]
  transfers between devices with their start and end apart: 4 -> 0, of which waited for: 4 -> 0; matrix products, arithmetic and copies ran while one was open for 11% -> 0% of each run, Pallas kernels for 0% -> 0%
where the time goes in v1:
time: 186 us; the launch traced here: 184 us
  Pallas kernels  184 us (99%)
    pallas_call x1, Pallas kernels, main_call(): pl.pallas_call(main_kernel, out_shape=jax.ShapeDtypeStruct((4, 4, B, B),...  173 us
    pallas_call x1, Pallas kernels, sum_call(): pl.pallas_call(sum_kernel, grid=(4, 2), out_shape=jax.ShapeDtypeStruct((4...  11.6 us

profile of v1, /device:TPU:1, one launch (start us, length us, event | category | flops | bytes accessed | tf_op | source)
XLA Modules:
  0.0 184.3 jit_solution(2124041053762587171)
XLA Ops:
  0.0 172.7 %gather_update_exchange.1.blocks = bf16[4,4,512,512]{3,2,1,0:T(8,128)(2,1)} custom-call(s32[32]{0:T(128)} %bitcast.11, s32[32]{0:T(128)} %bitcast.12, s32[8,16]{1,0:T(8,128)} %halves.3, s32[2,32]{1,0:T(2,128)} %shifts.3, bf16[512,1024]{1,0:T(8,128)(2,1)} %bitcast.7, bf16[512,1024]{1,0:T(8,128)(2,1)} %bitcast.8, bf16[512,1024]{1,0:T(8,128)(2,1)} %bitcast.9, ...), custom_call_target="tpu_custom_call" | custom-call | tf_op jit(solution)/shard_map/gather_update_exchange/pallas_call | solution.py:384
  172.7 11.6 %sum_into_slots.1 = bf16[4,4,512,512]{3,2,1,0:T(8,128)(2,1)} custom-call(s32[8,16]{1,0:T(8,128)} %halves.3, s32[2,32]{1,0:T(2,128)} %shifts.3, bf16[4,4,512,512]{3,2,1,0:T(8,128)(2,1)} %gather_update_exchange.1.blocks), custom_call_target="tpu_custom_call" | custom-call | tf_op jit(solution)/shard_map/sum_into_slots/pallas_call | solution.py:436

commit v2 on v1

v2 whole, which is shorter than its diff:
```python
import functools

import jax
import jax.numpy as jnp
from jax import lax
from jax.experimental import pallas as pl
from jax.experimental.pallas import tpu as pltpu
from jax.sharding import PartitionSpec as P

MESH = pl.DeviceIdType.MESH
B = 512
R = 32
KP = 32
K = 1024
CH = 4
PR = B // CH
HR = PR // 2
PK = K // CH
BF = jnp.bfloat16

Y_OPS = (
    [("Y", 0, 0, k) for k in range(CH)]
    + [("X", 0, 0, k) for k in range(CH)]
    + [("X", d, 0, k) for k in range(CH) for d in (1, -1)]
    + [("X", 2, 0, 1), ("X", 2, 0, 3)]
)


def x_ops(sign):
    a, b = (0, 1) if sign > 0 else (2, 3)
    return (
        [("Y", 0, 0, k) for k in range(CH)]
        + [("Y", 0, 1, 0), ("Y", 0, 1, 1)]
        + ([("Y", 0, 1, 2), ("X", 0, 0, 0)] if sign > 0 else [("X", 0, 0, 0), ("Y", 0, 1, 2)])
        + [("Y", 0, 1, 3)]
        + [("X", 0, 0, k) for k in range(1, CH)]
        + [("Y", -sign, 0, a), ("Y", -sign, 0, b), ("Y", -sign, 1, a)]
        + [("X", -sign, 0, b), ("Y", -sign, 1, b), ("X", -sign, 0, a), ("X", -sign, 1, a)]
    )


LINK_OPS = [("y",) + op for op in Y_OPS] + [("+",) + op for op in x_ops(1)] + [("-",) + op for op in x_ops(-1)]
LINK_ID = {op: i for i, op in enumerate(LINK_OPS)}
CORE_OPS = [(kind, dx, dy, k) for kind in "YX" for dx in (0, 1, -1, 2) for dy in (0, 1) for k in range(CH)]
CORE_ID = {op: i for i, op in enumerate(CORE_OPS)}
Z_STEPS = (
    [(0, k) for k in range(CH)]
    + [(d, k) for k in range(CH) for d in (1, -1)]
    + [(2, k) for k in (1, 3, 0, 2)]
)
V_SLOT = {0: 0, 1: 1, -1: 2, 2: 0}


def main_kernel(
    lrank, urank, halves, shifts, xin, yin, pin, qin, out,
    xbuf, ybuf, vbuf, pbuf, qtbuf, raw, stage, sbuf, relay,
    in_sem, ls, lr, cs, cr, zs, zr, zlast, os_sem,
):
    front, tile = lax.axis_index("front"), lax.axis_index("tile")
    yh, z = front // 4, front % 4
    x, yl, core = tile // 4, (tile // 2) % 2, tile % 2

    def tile_at(gx, gy, gc):
        return (gx * 2 + gy) * 2 + gc

    dev = {
        "y": (front, tile_at(x, 1 - yl, core)),
        "+": (front, tile_at((x + 1) % 4, yl, core)),
        "-": (front, tile_at((x + 3) % 4, yl, core)),
        "c": (front, tile_at(x, yl, 1 - core)),
        "z+": (yh * 4 + (z + 1) % 4, tile),
        "z-": (yh * 4 + (z + 3) % 4, tile),
    }

    def row_of(dx, dy, gc):
        gy = yl if dy == 0 else 1 - yl
        return tile_at((x + dx + 4) % 4, gy, gc)

    def piece(kind, dx, dy, gc, k):
        if kind == "X":
            return xbuf.at[row_of(dx, dy, gc), pl.ds(k * PR, PR), :]
        return ybuf.at[row_of(dx, dy, gc), pl.ds(k * PK, PK), :]

    def copy_of(ref, ssem, rsem, to):
        return pltpu.make_async_remote_copy(
            src_ref=ref, dst_ref=ref, send_sem=ssem, recv_sem=rsem,
            device_id=dev[to], device_id_type=MESH,
        )

    def send(link, kind, dx, dy, k):
        i = LINK_ID[(link, kind, dx, dy, k)]
        copy_of(piece(kind, dx, dy, core, k), ls, lr.at[i], link).start()

    def core_send(kind, dx, dy, k):
        i = CORE_ID[(kind, dx, dy, k)]
        copy_of(piece(kind, dx, dy, core, k), cs, cr.at[i], "c").start()

    def core_recv(kind, dx, dy, k):
        i = CORE_ID[(kind, dx, dy, k)]
        copy = copy_of(piece(kind, dx, dy, 1 - core, k), cs, cr.at[i], "c")
        copy.wait_recv()

    def recv(link, kind, dx, dy, k):
        if link == "y":
            sender = (kind, dx, 1 - dy, k)
        elif link == "+":
            sender = (kind, (dx + 2) % 4 - 1, dy, k)
        else:
            sender = (kind, dx % 4 - 1, dy, k)
        i = LINK_ID[(link,) + sender]
        copy = copy_of(piece(kind, dx, dy, core, k), ls, lr.at[i], link)
        copy.wait_recv()
        core_send(kind, dx, dy, k)

    me = tile
    y_loads = []
    for k in range(CH):
        cols = pl.ds(k * PK, PK)
        copy = pltpu.make_async_copy(yin.at[:, cols], raw.at[0, :, cols], in_sem.at[k])
        copy.start()
        y_loads.append(copy)
    x_load = pltpu.make_async_copy(xin, xbuf.at[me], in_sem.at[CH])
    p_load = pltpu.make_async_copy(pin, pbuf, in_sem.at[CH + 1])
    q_load = pltpu.make_async_copy(qin, raw.at[1], in_sem.at[CH + 2])
    x_load.start()
    p_load.start()
    q_load.start()

    barrier = pltpu.get_barrier_semaphore()
    for name in ("y", "+", "-", "c", "z+", "z-"):
        pl.semaphore_signal(barrier, inc=1, device_id=dev[name], device_id_type=MESH)

    col = lax.broadcasted_iota(jnp.int32, (8, K), 1)

    def keep(ranks):
        limit = jnp.zeros((8, K), jnp.int32)
        for k in range(KP):
            limit = jnp.where(col // R == k, ranks[k], limit)
        return (col % R < limit).astype(jnp.float32)[:1]

    lkeep = keep(lrank)

    def turn_y(k):
        y_loads[k].wait()
        part = raw[0, :, k * PK : (k + 1) * PK].astype(jnp.float32) * lkeep[:, k * PK : (k + 1) * PK]
        ybuf[me, k * PK : (k + 1) * PK, :] = part.T.astype(BF)

    def send_own_y(k):
        for link in ("y", "+", "-"):
            send(link, "Y", 0, 0, k)
        core_send("Y", 0, 0, k)

    turn_y(0)
    pl.semaphore_wait(barrier, 6)
    for k in range(1, CH):
        turn_y(k)
        send_own_y(k - 1)
    x_load.wait()
    send_own_y(CH - 1)
    for k in range(CH):
        send("y", "X", 0, 0, k)
        core_send("X", 0, 0, k)

    ukeep = keep(urank)
    p_load.wait()
    pbuf[...] = (pbuf[...].astype(jnp.float32) * ukeep).astype(BF)
    q_load.wait()
    for k in range(CH):
        cols = slice(k * PK, (k + 1) * PK)
        qtbuf[cols, :] = raw[1, :, cols].astype(jnp.float32).T.astype(BF)

    def make_v(dx, dy, k, classes=(0, 1)):
        slot = V_SLOT[dx]
        gy = yl if dy == 0 else 1 - yl
        rows = slice(k * PK, (k + 1) * PK)
        same = (
            lax.broadcasted_iota(jnp.int32, (PK, PK), 0) // R
            == lax.broadcasted_iota(jnp.int32, (PK, PK), 1) // R
        )
        cores = [core if c == 0 else 1 - core for c in classes]
        middles = []
        for gc in cores:
            m = jnp.dot(
                ybuf[row_of(dx, dy, gc), rows, :], pbuf[:, rows], preferred_element_type=jnp.float32
            )
            middles.append(jnp.where(same, m, 0.0).astype(BF))
        for gc, m in zip(cores, middles):
            v = jnp.dot(m, qtbuf[rows, :], preferred_element_type=jnp.float32)
            vbuf[slot, gy * 2 + gc, rows, :] = v.astype(BF)

    half = halves[front, tile]
    shift = shifts[yh, tile + 16 * half]

    def z_copy(n, what, src, dst, to):
        return pltpu.make_async_remote_copy(
            src_ref=src, dst_ref=dst, send_sem=zs, recv_sem=zr.at[n, what] if what < 2 else zlast,
            device_id=dev[to], device_id_type=MESH,
        )

    def z_refs(n, what, receiving=False):
        dx, k = Z_STEPS[n]
        g = (x + dx + 4) % 4
        back = (z + 3) % 4 if receiving else z
        ahead = (z + 1) % 4 if receiving else z
        if what == 0:
            return sbuf.at[n, 2, pl.ds(0, HR), :], relay.at[n, 0], "z+"
        if what == 1:
            return sbuf.at[n, 2, pl.ds(HR, HR), :], relay.at[n, 1], "z-"
        if what == 2:
            return sbuf.at[n, 1], out.at[back, g, pl.ds(k * PR, PR), :], "z+"
        if what == 3:
            return sbuf.at[n, 3], out.at[ahead, g, pl.ds(k * PR, PR), :], "z-"
        if what == 4:
            child = (z + 2) % 4 if receiving else (z + 3) % 4
            return relay.at[n, 0], out.at[child, g, pl.ds(k * PR, HR), :], "z+"
        child = (z + 2) % 4 if receiving else (z + 1) % 4
        return relay.at[n, 1], out.at[child, g, pl.ds(k * PR + HR, HR), :], "z-"

    def z_send(n, what):
        src, dst, to = z_refs(n, what)
        z_copy(n, what, src, dst, to).start()

    def z_wait(n, what):
        src, dst, to = z_refs(n, what, receiving=True)
        copy = z_copy(n, what, src, dst, to)
        copy.wait_recv()

    def hand_on(n):
        for what in (0, 1):
            z_wait(n, what)
            z_send(n, what + 4)

    def z_step(n):
        dx, k = Z_STEPS[n]
        slot = V_SLOT[dx]
        g = (x + dx + 4) % 4
        core_recv("X", dx, 0, k)
        core_recv("X", dx, 1, k)

        def body(r, carry):
            acc = jnp.dot(
                xbuf[g * 4 + r, pl.ds(k * PR, PR), :], vbuf[slot, r], preferred_element_type=jnp.float32
            )
            stage[r] = acc.astype(BF)
            return carry

        lax.fori_loop(0, 4, body, 0, unroll=2)
        for rel in (2, 1, 3, 0):
            sbuf[n, rel] = stage[(z + rel - shift + 4) % 4]
        for what in (0, 1, 2, 3):
            z_send(n, what)
        pltpu.make_async_copy(sbuf.at[n, 0], out.at[z, g, pl.ds(k * PR, PR), :], os_sem).start()

    def relay_of(n):
        if n >= 0:
            hand_on(n)

    for k in range(CH):
        core_recv("Y", 0, 0, k)
        make_v(0, 0, k)
    for k in range(CH):
        recv("y", "Y", 0, 1, k)
        send("+", "Y", 0, 1, k)
        send("-", "Y", 0, 1, k)
        if k == 1:
            send("-", "X", 0, 0, 0)
        if k == 2:
            send("+", "X", 0, 0, 0)
        if k == 3:
            for j in range(1, CH):
                send("+", "X", 0, 0, j)
                send("-", "X", 0, 0, j)
        recv("+", "Y", -1, 0, k)
        recv("-", "Y", 1, 0, k)
        core_recv("Y", 0, 1, k)
        make_v(0, 1, k)
        if k < 3:
            for d in (1, -1):
                core_recv("Y", d, 0, k)
                make_v(d, 0, k)
    for k in range(CH):
        recv("y", "X", 0, 1, k)
        if k == 2:
            recv("-", "X", 1, 0, 0)
            send("y", "X", 1, 0, 0)
        else:
            recv("-", "Y", 1, 1, min(k, 2))
        if k == 3:
            recv("+", "X", -1, 0, 0)
            send("y", "X", -1, 0, 0)
        else:
            recv("+", "Y", -1, 1, k)
        z_step(k)
        relay_of(k - 1)
        if k == 0:
            for d in (1, -1):
                core_recv("Y", d, 0, 3)
                make_v(d, 0, 3)
        if k < 3:
            core_recv("Y", -1, 1, k)
            make_v(-1, 1, k)
        if k != 2:
            core_recv("Y", 1, 1, min(k, 2))
            make_v(1, 1, min(k, 2))
    for u in range(8, 19):
        if u == 8:
            recv("-", "Y", 1, 1, 3)
            recv("+", "Y", -1, 1, 3)
            core_recv("Y", 1, 1, 3)
            make_v(1, 1, 3)
            for d, sign, a, b in ((-1, "+", 0, 1), (1, "-", 2, 3)):
                send(sign, "Y", d, 0, a)
                send(sign, "Y", d, 0, b)
                send(sign, "Y", d, 1, a)
        elif u <= 11:
            k = u - 8
            recv("-", "X", 1, 0, k)
            send("y", "X", 1, 0, k)
            recv("+", "X", -1, 0, k)
            send("y", "X", -1, 0, k)
            if k == 1:
                send("+", "X", -1, 0, 1)
                send("+", "Y", -1, 1, 1)
                send("+", "X", -1, 0, 0)
            if k == 3:
                send("-", "X", 1, 0, 3)
                send("-", "Y", 1, 1, 3)
                send("-", "X", 1, 0, 2)
        elif u <= 13:
            recv("+", "Y", 2, 0, u - 12)
            recv("-", "Y", 2, 0, u - 10)
        elif u == 14:
            recv("+", "Y", 2, 1, 0)
            recv("-", "Y", 2, 1, 2)
        elif u == 15:
            recv("+", "X", 2, 0, 1)
            send("y", "X", 2, 0, 1)
            recv("-", "X", 2, 0, 3)
            send("y", "X", 2, 0, 3)
        elif u == 16:
            recv("+", "Y", 2, 1, 1)
            recv("-", "Y", 2, 1, 3)
        elif u == 17:
            recv("+", "X", 2, 0, 0)
            recv("-", "X", 2, 0, 2)
        else:
            recv("+", "X", 2, 1, 0)
            recv("-", "X", 2, 1, 2)
        if u < 16:
            d, k = Z_STEPS[u - 4]
            recv("y", "X", d, 1, k)
            if (d, k) == (-1, 0):
                send("+", "X", -1, 1, 0)
            if (d, k) == (1, 2):
                send("-", "X", 1, 1, 2)
        elif u < 18:
            recv("y", "X", 2, 1, 1 if u == 16 else 3)
        if u == 16:
            for k in (1, 3):
                core_recv("Y", 2, 1, k)
                make_v(2, 1, k)
        z_step(u - 4)
        if u < 18:
            relay_of(u - 5)
        if u == 8:
            core_recv("Y", -1, 1, 3)
            make_v(-1, 1, 3)
        if u in (13, 14):
            for k in (0, 2) if u == 13 else (1, 3):
                core_recv("Y", 2, 0, k)
                make_v(2, 0, k)
        if u == 15:
            for k in (0, 2):
                core_recv("Y", 2, 1, k)
                make_v(2, 1, k)
    z_step(4 * CH - 1)
    for n in (13, 14, 15):
        hand_on(n)
    theirs = out.at[pl.ds(0, 3)]
    z_all = pltpu.make_async_remote_copy(
        src_ref=sbuf, dst_ref=theirs, send_sem=zs, recv_sem=zlast, device_id=dev["z+"], device_id_type=MESH
    )
    z_all.wait_recv()
    pltpu.make_async_copy(out.at[0], out.at[0], os_sem).wait()
    copy_of(xbuf.at[pl.ds(0, len(LINK_OPS) // CH)], ls, lr.at[0], "y").wait_send()
    copy_of(xbuf, cs, cr.at[0], "c").wait_send()
    copy_of(sbuf, zs, zlast, "z+").wait_send()


def main_call(xin, yin, pin, qin, lrank, urank, halves, shifts):
    hbm = pl.BlockSpec(memory_space=pl.ANY)
    smem = pl.BlockSpec(memory_space=pltpu.SMEM)
    steps = 4 * CH
    return pl.pallas_call(
        main_kernel,
        out_shape=jax.ShapeDtypeStruct((4, 4, B, B), BF),
        in_specs=[smem] * 4 + [hbm] * 4,
        out_specs=hbm,
        scratch_shapes=[
            pltpu.VMEM((16, B, K), BF),
            pltpu.VMEM((16, K, B), BF),
            pltpu.VMEM((3, 4, K, B), BF),
            pltpu.VMEM((B, K), BF),
            pltpu.VMEM((K, B), BF),
            pltpu.VMEM((2, B, K), BF),
            pltpu.VMEM((4, PR, B), BF),
            pltpu.VMEM((steps, 4, PR, B), BF),
            pltpu.VMEM((steps, 2, HR, B), BF),
            pltpu.SemaphoreType.DMA((CH + 3,)),
            pltpu.SemaphoreType.DMA,
            pltpu.SemaphoreType.DMA((len(LINK_OPS),)),
            pltpu.SemaphoreType.DMA,
            pltpu.SemaphoreType.DMA((len(CORE_OPS),)),
            pltpu.SemaphoreType.DMA,
            pltpu.SemaphoreType.DMA((steps, 2)),
            pltpu.SemaphoreType.DMA,
            pltpu.SemaphoreType.DMA,
        ],
        compiler_params=pltpu.CompilerParams(
            collective_id=0, has_side_effects=True, vmem_limit_bytes=64_000_000
        ),
        name="gather_update_exchange",
    )(lrank, urank, halves, shifts, xin, yin, pin, qin)


def sum_kernel(halves, shifts, blocks, out):
    front, tile = lax.axis_index("front"), lax.axis_index("tile")
    parent, o = front // 4, front % 4
    g = pl.program_id(0)
    place = []
    for c in range(4):
        child = 4 * parent + c
        col_half = halves[child, tile]
        row = 4 * g + (o - shifts[parent, tile + 16 * col_half] + 4) % 4
        place.append(2 * col_half + halves[child, row])
    for s in range(4):
        count = sum((place[c] == s).astype(jnp.int32) for c in range(4))
        only = sum(jnp.where(place[c] == s, c, 0) for c in range(4))

        @pl.when(count == 0)
        def _():
            out[s, 0] = jnp.zeros(out.shape[2:], BF)

        @pl.when(count == 1)
        def _():
            out[s, 0] = blocks[only, 0]

        @pl.when(count > 1)
        def _():
            total = jnp.zeros(blocks.shape[2:], jnp.float32)
            for c in range(4):
                total = total + jnp.where(place[c] == s, blocks[c, 0].astype(jnp.float32), 0.0)
            out[s, 0] = total.astype(BF)


def sum_call(halves, shifts, blocks):
    rows = B // 2
    smem = pl.BlockSpec(memory_space=pltpu.SMEM)
    block = pl.BlockSpec((4, 1, rows, B), lambda g, i: (0, g, i, 0))
    return pl.pallas_call(
        sum_kernel,
        grid=(4, 2),
        out_shape=jax.ShapeDtypeStruct((4, 4, B, B), BF),
        in_specs=[smem, smem, block],
        out_specs=block,
        name="sum_into_slots",
    )(halves, shifts, blocks)


def per_device(lower_basis, lower_coeff, upper_basis, upper_coeff, lower_rank, upper_rank, child_half, owner_shift):
    blocks = main_call(
        lower_basis[0, 0], lower_coeff[0, 0], upper_basis[0, 0], upper_coeff[0, 0],
        lower_rank[0, 0], upper_rank[0, 0], child_half, owner_shift,
    )
    return sum_call(child_half, owner_shift, blocks).reshape(1, 1, 16 * B, B)


def solution(mesh):
    whole = P("front", "tile", None, None)
    ranks = P("front", "tile", None)
    return jax.shard_map(
        per_device,
        mesh=mesh,
        in_specs=(whole, whole, whole, whole, ranks, ranks, P(), P()),
        out_specs=whole,
        check_vma=False,
    )
```

time: 186 us -> 149 us (0.80)
  Pallas kernels: 184 us -> 149 us
    pallas_call x1, Pallas kernels: 173 us -> 139 us  [main_call(): pl.pallas_call(main_kernel, out_shape=jax.ShapeDtypeStruct((4, 4, B, B),...]
where the time goes in v2:
time: 149 us
  Pallas kernels  149 us (100%)
    pallas_call x1, Pallas kernels, main_call(): pl.pallas_call(main_kernel, out_shape=jax.ShapeDtypeStruct((4, 4, B, B),...  139 us
    pallas_call x1, Pallas kernels, sum_call(): pl.pallas_call(sum_kernel, grid=(4, 2), out_shape=jax.ShapeDtypeStruct((4...  10.2 us

profile of v2, /device:TPU:1, one launch (start us, length us, event | category | flops | bytes accessed | tf_op | source)
XLA Modules:
  0.0 148.9 jit_solution(9920622654802236121)
XLA Ops:
  0.0 138.6 %gather_update_exchange.1.blocks = bf16[4,4,512,512]{3,2,1,0:T(8,128)(2,1)} custom-call(s32[32]{0:T(128)} %bitcast.11, s32[32]{0:T(128)} %bitcast.12, s32[8,16]{1,0:T(8,128)} %halves.3, s32[2,32]{1,0:T(2,128)} %shifts.3, bf16[512,1024]{1,0:T(8,128)(2,1)} %bitcast.7, bf16[512,1024]{1,0:T(8,128)(2,1)} %bitcast.8, bf16[512,1024]{1,0:T(8,128)(2,1)} %bitcast.9, ...), custom_call_target="tpu_custom_call" | custom-call | tf_op jit(solution)/shard_map/gather_update_exchange/pallas_call | solution.py:394
  138.6 10.2 %sum_into_slots.1 = bf16[4,4,512,512]{3,2,1,0:T(8,128)(2,1)} custom-call(s32[8,16]{1,0:T(8,128)} %halves.3, s32[2,32]{1,0:T(2,128)} %shifts.3, bf16[4,4,512,512]{3,2,1,0:T(8,128)(2,1)} %gather_update_exchange.1.blocks), custom_call_target="tpu_custom_call" | custom-call | tf_op jit(solution)/shard_map/sum_into_slots/pallas_call | solution.py:460

commit v3 on v2

--- a/solution.py
+++ b/solution.py
@@ -31,11 +31,14 @@
     return (
         [("Y", 0, 0, k) for k in range(CH)]
         + [("Y", 0, 1, 0), ("Y", 0, 1, 1)]
-        + ([("Y", 0, 1, 2), ("X", 0, 0, 0)] if sign > 0 else [("X", 0, 0, 0), ("Y", 0, 1, 2)])
-        + [("Y", 0, 1, 3)]
-        + [("X", 0, 0, k) for k in range(1, CH)]
-        + [("Y", -sign, 0, a), ("Y", -sign, 0, b), ("Y", -sign, 1, a)]
-        + [("X", -sign, 0, b), ("Y", -sign, 1, b), ("X", -sign, 0, a), ("X", -sign, 1, a)]
+        + (
+            [("Y", 0, 1, 2), ("X", 0, 0, 0), ("X", 0, 0, 1), ("Y", 0, 1, 3)]
+            if sign > 0
+            else [("X", 0, 0, 0), ("Y", 0, 1, 2), ("Y", 0, 1, 3), ("X", 0, 0, 1)]
+        )
+        + [("X", 0, 0, 2), ("X", 0, 0, 3)]
+        + [("Y", -sign, 0, a), ("Y", -sign, 0, b), ("X", -sign, 0, b)]
+        + [("Y", -sign, 1, a), ("Y", -sign, 1, b), ("X", -sign, 0, a), ("X", -sign, 1, a)]
     )
 
 
@@ -45,7 +48,7 @@
 CORE_ID = {op: i for i, op in enumerate(CORE_OPS)}
 Z_STEPS = (
     [(0, k) for k in range(CH)]
-    + [(d, k) for k in range(CH) for d in (1, -1)]
+    + [(1, 0), (-1, 0), (-1, 1), (1, 1), (1, 2), (-1, 2), (1, 3), (-1, 3)]
     + [(2, k) for k in (1, 3, 0, 2)]
 )
 V_SLOT = {0: 0, 1: 1, -1: 2, 2: 0}
@@ -53,8 +56,8 @@
 
 def main_kernel(
     lrank, urank, halves, shifts, xin, yin, pin, qin, out,
-    xbuf, ybuf, vbuf, pbuf, qtbuf, raw, stage, sbuf, relay,
-    in_sem, ls, lr, cs, cr, zs, zr, zlast, os_sem,
+    xbuf, ybuf, vbuf, pbuf, qtbuf, stage, sbuf, relay,
+    in_sem, ls, lr, cs, cr, zs, zr, zlast,
 ):
     front, tile = lax.axis_index("front"), lax.axis_index("tile")
     yh, z = front // 4, front % 4
@@ -113,18 +116,24 @@
         core_send(kind, dx, dy, k)
 
     me = tile
+
+    def raw(n, k):
+        return vbuf.at[2, n, pl.ds(k // 2 * B, B), pl.ds(k % 2 * PK, PK)]
+
     y_loads = []
     for k in range(CH):
         cols = pl.ds(k * PK, PK)
-        copy = pltpu.make_async_copy(yin.at[:, cols], raw.at[0, :, cols], in_sem.at[k])
+        copy = pltpu.make_async_copy(yin.at[:, cols], raw(0, k), in_sem.at[k])
         copy.start()
         y_loads.append(copy)
     x_load = pltpu.make_async_copy(xin, xbuf.at[me], in_sem.at[CH])
     p_load = pltpu.make_async_copy(pin, pbuf, in_sem.at[CH + 1])
-    q_load = pltpu.make_async_copy(qin, raw.at[1], in_sem.at[CH + 2])
-    x_load.start()
-    p_load.start()
-    q_load.start()
+    q_loads = [
+        pltpu.make_async_copy(qin.at[:, pl.ds(k * PK, PK)], raw(1, k), in_sem.at[CH + 2 + k])
+        for k in range(CH)
+    ]
+    for copy in [x_load, p_load] + q_loads:
+        copy.start()
 
     barrier = pltpu.get_barrier_semaphore()
     for name in ("y", "+", "-", "c", "z+", "z-"):
@@ -142,7 +151,7 @@
 
     def turn_y(k):
         y_loads[k].wait()
-        part = raw[0, :, k * PK : (k + 1) * PK].astype(jnp.float32) * lkeep[:, k * PK : (k + 1) * PK]
+        part = raw(0, k)[...].astype(jnp.float32) * lkeep[:, k * PK : (k + 1) * PK]
         ybuf[me, k * PK : (k + 1) * PK, :] = part.T.astype(BF)
 
     def send_own_y(k):
@@ -164,10 +173,9 @@
     ukeep = keep(urank)
     p_load.wait()
     pbuf[...] = (pbuf[...].astype(jnp.float32) * ukeep).astype(BF)
-    q_load.wait()
-    for k in range(CH):
-        cols = slice(k * PK, (k + 1) * PK)
-        qtbuf[cols, :] = raw[1, :, cols].astype(jnp.float32).T.astype(BF)
+    for k in range(CH):
+        q_loads[k].wait()
+        qtbuf[k * PK : (k + 1) * PK, :] = raw(1, k)[...].astype(jnp.float32).T.astype(BF)
 
     def make_v(dx, dy, k, classes=(0, 1)):
         slot = V_SLOT[dx]
@@ -188,42 +196,63 @@
             v = jnp.dot(m, qtbuf[rows, :], preferred_element_type=jnp.float32)
             vbuf[slot, gy * 2 + gc, rows, :] = v.astype(BF)
 
+    col_half = [halves[4 * yh + c, tile] for c in range(4)]
+    col_shift = [shifts[yh, tile + 16 * col_half[c]] for c in range(4)]
     half = halves[front, tile]
     shift = shifts[yh, tile + 16 * half]
 
     def z_copy(n, what, src, dst, to):
         return pltpu.make_async_remote_copy(
-            src_ref=src, dst_ref=dst, send_sem=zs, recv_sem=zr.at[n, what] if what < 2 else zlast,
+            src_ref=src, dst_ref=dst, send_sem=zs, recv_sem=zr.at[n, what] if what < 2 else zlast.at[n],
             device_id=dev[to], device_id_type=MESH,
         )
 
-    def z_refs(n, what, receiving=False):
+    def z_refs(n, what):
         dx, k = Z_STEPS[n]
         g = (x + dx + 4) % 4
-        back = (z + 3) % 4 if receiving else z
-        ahead = (z + 1) % 4 if receiving else z
         if what == 0:
-            return sbuf.at[n, 2, pl.ds(0, HR), :], relay.at[n, 0], "z+"
+            return sbuf.at[n, 1, pl.ds(0, HR), :], relay.at[n, 0], "z+"
         if what == 1:
-            return sbuf.at[n, 2, pl.ds(HR, HR), :], relay.at[n, 1], "z-"
+            return sbuf.at[n, 1, pl.ds(HR, HR), :], relay.at[n, 1], "z-"
         if what == 2:
-            return sbuf.at[n, 1], out.at[back, g, pl.ds(k * PR, PR), :], "z+"
+            return sbuf.at[n, 0], out.at[z, g, pl.ds(k * PR, PR), :], "z+"
         if what == 3:
-            return sbuf.at[n, 3], out.at[ahead, g, pl.ds(k * PR, PR), :], "z-"
+            return sbuf.at[n, 2], out.at[z, g, pl.ds(k * PR, PR), :], "z-"
         if what == 4:
-            child = (z + 2) % 4 if receiving else (z + 3) % 4
-            return relay.at[n, 0], out.at[child, g, pl.ds(k * PR, HR), :], "z+"
-        child = (z + 2) % 4 if receiving else (z + 1) % 4
-        return relay.at[n, 1], out.at[child, g, pl.ds(k * PR + HR, HR), :], "z-"
+            return relay.at[n, 0], out.at[(z + 3) % 4, g, pl.ds(k * PR, HR), :], "z+"
+        return relay.at[n, 1], out.at[(z + 1) % 4, g, pl.ds(k * PR + HR, HR), :], "z-"
 
     def z_send(n, what):
         src, dst, to = z_refs(n, what)
         z_copy(n, what, src, dst, to).start()
 
     def z_wait(n, what):
-        src, dst, to = z_refs(n, what, receiving=True)
+        src, dst, to = z_refs(n, what)
         copy = z_copy(n, what, src, dst, to)
         copy.wait_recv()
+
+    def sum_step(n):
+        dx, k = Z_STEPS[n]
+        g = (x + dx + 4) % 4
+        copy = z_copy(n, 2, sbuf.at[n], out.at[pl.ds(0, 3), g, pl.ds(k * PR, PR), :], "z+")
+        copy.wait_recv()
+        place = []
+        for c in range(4):
+            row = 4 * g + (z - col_shift[c] + 4) % 4
+            place.append(2 * col_half[c] + halves[4 * yh + c, row])
+        depth = 16
+
+        def body(i, carry):
+            rows = pl.ds(pl.multiple_of(k * PR + i * depth, depth), depth)
+            tiles = [out[c, g, rows, :].astype(jnp.float32) for c in range(4)]
+            for s in range(4):
+                total = jnp.zeros((depth, B), jnp.float32)
+                for c in range(4):
+                    total = total + jnp.where(place[c] == s, tiles[c], 0.0)
+                out[s, g, rows, :] = total.astype(BF)
+            return carry
+
+        lax.fori_loop(0, PR // depth, body, 0)
 
     def hand_on(n):
         for what in (0, 1):
@@ -245,11 +274,11 @@
             return carry
 
         lax.fori_loop(0, 4, body, 0, unroll=2)
-        for rel in (2, 1, 3, 0):
-            sbuf[n, rel] = stage[(z + rel - shift + 4) % 4]
+        for rel in (2, 1, 3):
+            sbuf[n, rel - 1] = stage[(z + rel - shift + 4) % 4]
         for what in (0, 1, 2, 3):
             z_send(n, what)
-        pltpu.make_async_copy(sbuf.at[n, 0], out.at[z, g, pl.ds(k * PR, PR), :], os_sem).start()
+        out[z, g, pl.ds(k * PR, PR), :] = stage[(z - shift + 4) % 4]
 
     def relay_of(n):
         if n >= 0:
@@ -266,10 +295,12 @@
             send("-", "X", 0, 0, 0)
         if k == 2:
             send("+", "X", 0, 0, 0)
+            send("+", "X", 0, 0, 1)
         if k == 3:
             for j in range(1, CH):
-                send("+", "X", 0, 0, j)
                 send("-", "X", 0, 0, j)
+                if j > 1:
+                    send("+", "X", 0, 0, j)
         recv("+", "Y", -1, 0, k)
         recv("-", "Y", 1, 0, k)
         core_recv("Y", 0, 1, k)
@@ -305,41 +336,40 @@
     for u in range(8, 19):
         if u == 8:
             recv("-", "Y", 1, 1, 3)
-            recv("+", "Y", -1, 1, 3)
-            core_recv("Y", 1, 1, 3)
-            make_v(1, 1, 3)
+            recv("+", "X", -1, 0, 1)
+            send("y", "X", -1, 0, 1)
             for d, sign, a, b in ((-1, "+", 0, 1), (1, "-", 2, 3)):
                 send(sign, "Y", d, 0, a)
                 send(sign, "Y", d, 0, b)
-                send(sign, "Y", d, 1, a)
+            send("+", "X", -1, 0, 1)
+            send("+", "Y", -1, 1, 0)
         elif u <= 11:
             k = u - 8
             recv("-", "X", 1, 0, k)
             send("y", "X", 1, 0, k)
-            recv("+", "X", -1, 0, k)
-            send("y", "X", -1, 0, k)
             if k == 1:
-                send("+", "X", -1, 0, 1)
+                recv("+", "Y", -1, 1, 3)
                 send("+", "Y", -1, 1, 1)
                 send("+", "X", -1, 0, 0)
+            else:
+                recv("+", "X", -1, 0, k)
+                send("y", "X", -1, 0, k)
             if k == 3:
                 send("-", "X", 1, 0, 3)
+                send("-", "Y", 1, 1, 2)
                 send("-", "Y", 1, 1, 3)
                 send("-", "X", 1, 0, 2)
         elif u <= 13:
             recv("+", "Y", 2, 0, u - 12)
             recv("-", "Y", 2, 0, u - 10)
         elif u == 14:
-            recv("+", "Y", 2, 1, 0)
-            recv("-", "Y", 2, 1, 2)
-        elif u == 15:
             recv("+", "X", 2, 0, 1)
             send("y", "X", 2, 0, 1)
             recv("-", "X", 2, 0, 3)
             send("y", "X", 2, 0, 3)
-        elif u == 16:
-            recv("+", "Y", 2, 1, 1)
-            recv("-", "Y", 2, 1, 3)
+        elif u <= 16:
+            recv("+", "Y", 2, 1, u - 15)
+            recv("-", "Y", 2, 1, u - 13)
         elif u == 17:
             recv("+", "X", 2, 0, 0)
             recv("-", "X", 2, 0, 2)
@@ -355,6 +385,12 @@
                 send("-", "X", 1, 1, 2)
         elif u < 18:
             recv("y", "X", 2, 1, 1 if u == 16 else 3)
+        if u == 8:
+            core_recv("Y", 1, 1, 3)
+            make_v(1, 1, 3)
+        if u == 9:
+            core_recv("Y", -1, 1, 3)
+            make_v(-1, 1, 3)
         if u == 16:
             for k in (1, 3):
                 core_recv("Y", 2, 1, k)
@@ -362,11 +398,9 @@
         z_step(u - 4)
         if u < 18:
             relay_of(u - 5)
-        if u == 8:
-            core_recv("Y", -1, 1, 3)
-            make_v(-1, 1, 3)
-        if u in (13, 14):
-            for k in (0, 2) if u == 13 else (1, 3):
+            sum_step(u - 8)
+        if u in (12, 13):
+            for k in (0, 2) if u == 12 else (1, 3):
                 core_recv("Y", 2, 0, k)
                 make_v(2, 0, k)
         if u == 15:
@@ -376,15 +410,12 @@
     z_step(4 * CH - 1)
     for n in (13, 14, 15):
         hand_on(n)
-    theirs = out.at[pl.ds(0, 3)]
-    z_all = pltpu.make_async_remote_copy(
-        src_ref=sbuf, dst_ref=theirs, send_sem=zs, recv_sem=zlast, device_id=dev["z+"], device_id_type=MESH
-    )
-    z_all.wait_recv()
-    pltpu.make_async_copy(out.at[0], out.at[0], os_sem).wait()
+        sum_step(n - 3)
+    for n in (13, 14, 15):
+        sum_step(n)
     copy_of(xbuf.at[pl.ds(0, len(LINK_OPS) // CH)], ls, lr.at[0], "y").wait_send()
     copy_of(xbuf, cs, cr.at[0], "c").wait_send()
-    copy_of(sbuf, zs, zlast, "z+").wait_send()
+    copy_of(out, zs, zlast.at[0], "z+").wait_send()
 
 
 def main_call(xin, yin, pin, qin, lrank, urank, halves, shifts):
@@ -393,78 +424,32 @@
     steps = 4 * CH
     return pl.pallas_call(
         main_kernel,
-        out_shape=jax.ShapeDtypeStruct((4, 4, B, B), BF),
+        out_shape=pltpu.VMEM((4, 4, B, B), BF),
         in_specs=[smem] * 4 + [hbm] * 4,
-        out_specs=hbm,
+        out_specs=pl.BlockSpec(memory_space=pltpu.VMEM),
         scratch_shapes=[
             pltpu.VMEM((16, B, K), BF),
             pltpu.VMEM((16, K, B), BF),
             pltpu.VMEM((3, 4, K, B), BF),
             pltpu.VMEM((B, K), BF),
             pltpu.VMEM((K, B), BF),
-            pltpu.VMEM((2, B, K), BF),
             pltpu.VMEM((4, PR, B), BF),
-            pltpu.VMEM((steps, 4, PR, B), BF),
+            pltpu.VMEM((steps, 3, PR, B), BF),
             pltpu.VMEM((steps, 2, HR, B), BF),
-            pltpu.SemaphoreType.DMA((CH + 3,)),
+            pltpu.SemaphoreType.DMA((2 * CH + 2,)),
             pltpu.SemaphoreType.DMA,
             pltpu.SemaphoreType.DMA((len(LINK_OPS),)),
             pltpu.SemaphoreType.DMA,
             pltpu.SemaphoreType.DMA((len(CORE_OPS),)),
             pltpu.SemaphoreType.DMA,
             pltpu.SemaphoreType.DMA((steps, 2)),
-            pltpu.SemaphoreType.DMA,
-            pltpu.SemaphoreType.DMA,
+            pltpu.SemaphoreType.DMA((steps,)),
         ],
         compiler_params=pltpu.CompilerParams(
-            collective_id=0, has_side_effects=True, vmem_limit_bytes=64_000_000
+            collective_id=0, has_side_effects=True, vmem_limit_bytes=58_000_000
         ),
         name="gather_update_exchange",
     )(lrank, urank, halves, shifts, xin, yin, pin, qin)
-
-
-def sum_kernel(halves, shifts, blocks, out):
-    front, tile = lax.axis_index("front"), lax.axis_index("tile")
-    parent, o = front // 4, front % 4
-    g = pl.program_id(0)
-    place = []
-    for c in range(4):
-        child = 4 * parent + c
-        col_half = halves[child, tile]
-        row = 4 * g + (o - shifts[parent, tile + 16 * col_half] + 4) % 4
-        place.append(2 * col_half + halves[child, row])
-    for s in range(4):
-        count = sum((place[c] == s).astype(jnp.int32) for c in range(4))
-        only = sum(jnp.where(place[c] == s, c, 0) for c in range(4))
-
-        @pl.when(count == 0)
-        def _():
-            out[s, 0] = jnp.zeros(out.shape[2:], BF)
-
-        @pl.when(count == 1)
-        def _():
-            out[s, 0] = blocks[only, 0]
-
-        @pl.when(count > 1)
-        def _():
-            total = jnp.zeros(blocks.shape[2:], jnp.float32)
-            for c in range(4):
-                total = total + jnp.where(place[c] == s, blocks[c, 0].astype(jnp.float32), 0.0)
-            out[s, 0] = total.astype(BF)
-
-
-def sum_call(halves, shifts, blocks):
-    rows = B // 2
-    smem = pl.BlockSpec(memory_space=pltpu.SMEM)
-    block = pl.BlockSpec((4, 1, rows, B), lambda g, i: (0, g, i, 0))
-    return pl.pallas_call(
-        sum_kernel,
-        grid=(4, 2),
-        out_shape=jax.ShapeDtypeStruct((4, 4, B, B), BF),
-        in_specs=[smem, smem, block],
-        out_specs=block,
-        name="sum_into_slots",
-    )(halves, shifts, blocks)
 
 
 def per_device(lower_basis, lower_coeff, upper_basis, upper_coeff, lower_rank, upper_rank, child_half, owner_shift):
@@ -472,7 +457,7 @@
         lower_basis[0, 0], lower_coeff[0, 0], upper_basis[0, 0], upper_coeff[0, 0],
         lower_rank[0, 0], upper_rank[0, 0], child_half, owner_shift,
     )
-    return sum_call(child_half, owner_shift, blocks).reshape(1, 1, 16 * B, B)
+    return blocks.reshape(1, 1, 16 * B, B)
 
 
 def solution(mesh):

time: 149 us -> 140 us (0.940)
  Pallas kernels: 149 us -> 137 us
  local copies, waits for them, and re-layouts: 0 us -> 3.4 us
    pallas_call x2 -> x1, Pallas kernels: 149 us -> 137 us  [main_call(): pl.pallas_call(main_kernel, out_shape=pltpu.VMEM((4, 4, B, B), BF), in_sp...]
    unnamed x0 -> x1, local copies, waits for them, and re-layouts: none -> 3.4 us
where the time goes in v3:
time: 140 us
  Pallas kernels  137 us (98%)
  local copies, waits for them, and re-layouts  3.4 us (2%)
    pallas_call x1, Pallas kernels, main_call(): pl.pallas_call(main_kernel, out_shape=pltpu.VMEM((4, 4, B, B), BF), in_sp...  137 us
    unnamed x1, local copies, waits for them, and re-layouts  3.4 us

profile of v3, /device:TPU:1, one launch (start us, length us, event | category | flops | bytes accessed | tf_op | source)
XLA Modules:
  0.0 140.1 jit_solution(2130711207708889611)
XLA Ops:
  0.0 136.7 %gather_update_exchange.1 = bf16[4,4,512,512]{3,2,1,0:T(8,128)(2,1)S(1)} custom-call(s32[32]{0:T(128)} %bitcast.12, s32[32]{0:T(128)} %bitcast.13, s32[8,16]{1,0:T(8,128)} %halves.1, s32[2,32]{1,0:T(2,128)} %shifts.1, bf16[512,1024]{1,0:T(8,128)(2,1)} %bitcast.8, bf16[512,1024]{1,0:T(8,128)(2,1)} %bitcast.9, bf16[512,1024]{1,0:T(8,128)(2,1)} %bitcast.10, ...), custom_call_target="tpu_custom_call" | custom-call | tf_op jit(solution)/shard_map/gather_update_exchange/pallas_call | solution.py:425
  136.7 3.4 %copy.10 = bf16[1,1,8192,512]{3,2,1,0:T(8,128)(2,1)} copy(bf16[1,1,8192,512]{3,2,1,0:T(8,128)(2,1)S(1)} %bitcast.7) | data formatting | bytes 16777216

commit v4 on v3

--- a/solution.py
+++ b/solution.py
@@ -14,15 +14,29 @@
 K = 1024
 CH = 4
 PR = B // CH
-HR = PR // 2
+SR = PR // 2
+HR = SR // 2
 PK = K // CH
 BF = jnp.bfloat16
 
+ALL = 20
+
+
+def halves_of(k):
+    return (10 + 2 * k, 11 + 2 * k)
+
+
+def rows_of(k):
+    if k == ALL:
+        return 0, B
+    return ((k - 10) * SR, SR) if k >= 10 else (k * PR, PR)
+
+
 Y_OPS = (
     [("Y", 0, 0, k) for k in range(CH)]
-    + [("X", 0, 0, k) for k in range(CH)]
-    + [("X", d, 0, k) for k in range(CH) for d in (1, -1)]
-    + [("X", 2, 0, 1), ("X", 2, 0, 3)]
+    + [("X", 0, 0, 10 + k) for k in range(2 * CH)]
+    + [("X", d, 0, 10 + k) for d in (1, -1) for k in range(2 * CH)]
+    + [("X", 2, 0, h) for k in (1, 3) for h in halves_of(k)]
 )
 
 
@@ -30,13 +44,8 @@
     a, b = (0, 1) if sign > 0 else (2, 3)
     return (
         [("Y", 0, 0, k) for k in range(CH)]
-        + [("Y", 0, 1, 0), ("Y", 0, 1, 1)]
-        + (
-            [("Y", 0, 1, 2), ("X", 0, 0, 0), ("X", 0, 0, 1), ("Y", 0, 1, 3)]
-            if sign > 0
-            else [("X", 0, 0, 0), ("Y", 0, 1, 2), ("Y", 0, 1, 3), ("X", 0, 0, 1)]
-        )
-        + [("X", 0, 0, 2), ("X", 0, 0, 3)]
+        + [("Y", 0, 1, k) for k in range(CH)]
+        + [("X", 0, 0, k) for k in range(CH)]
         + [("Y", -sign, 0, a), ("Y", -sign, 0, b), ("X", -sign, 0, b)]
         + [("Y", -sign, 1, a), ("Y", -sign, 1, b), ("X", -sign, 0, a), ("X", -sign, 1, a)]
     )
@@ -44,9 +53,15 @@
 
 LINK_OPS = [("y",) + op for op in Y_OPS] + [("+",) + op for op in x_ops(1)] + [("-",) + op for op in x_ops(-1)]
 LINK_ID = {op: i for i, op in enumerate(LINK_OPS)}
-CORE_OPS = [(kind, dx, dy, k) for kind in "YX" for dx in (0, 1, -1, 2) for dy in (0, 1) for k in range(CH)]
+CORE_OPS = (
+    [("Y", dx, dy, k) for dx in (0, 1, -1, 2) for dy in (0, 1) for k in range(CH)]
+    + [("X", 0, 0, ALL)]
+    + [("X", dx, 1, 10 + k) for dx in (0, 1, -1) for k in range(2 * CH)]
+    + [("X", dx, 0, k) for dx in (1, -1, 2) for k in range(CH)]
+    + [("X", 2, 1, k) for k in (0, 2) + halves_of(1) + halves_of(3)]
+)
 CORE_ID = {op: i for i, op in enumerate(CORE_OPS)}
-Z_STEPS = (
+Z_PAIRS = (
     [(0, k) for k in range(CH)]
     + [(1, 0), (-1, 0), (-1, 1), (1, 1), (1, 2), (-1, 2), (1, 3), (-1, 3)]
     + [(2, k) for k in (1, 3, 0, 2)]
@@ -81,7 +96,7 @@
 
     def piece(kind, dx, dy, gc, k):
         if kind == "X":
-            return xbuf.at[row_of(dx, dy, gc), pl.ds(k * PR, PR), :]
+            return xbuf.at[row_of(dx, dy, gc), pl.ds(*rows_of(k)), :]
         return ybuf.at[row_of(dx, dy, gc), pl.ds(k * PK, PK), :]
 
     def copy_of(ref, ssem, rsem, to):
@@ -160,15 +175,16 @@
         core_send("Y", 0, 0, k)
 
     turn_y(0)
+    turn_y(1)
     pl.semaphore_wait(barrier, 6)
-    for k in range(1, CH):
-        turn_y(k)
-        send_own_y(k - 1)
+    for k in range(CH):
+        send_own_y(k)
+        if k + 2 < CH:
+            turn_y(k + 2)
     x_load.wait()
-    send_own_y(CH - 1)
-    for k in range(CH):
-        send("y", "X", 0, 0, k)
-        core_send("X", 0, 0, k)
+    for k in range(2 * CH):
+        send("y", "X", 0, 0, 10 + k)
+    core_send("X", 0, 0, ALL)
 
     ukeep = keep(urank)
     p_load.wait()
@@ -203,38 +219,38 @@
 
     def z_copy(n, what, src, dst, to):
         return pltpu.make_async_remote_copy(
-            src_ref=src, dst_ref=dst, send_sem=zs, recv_sem=zr.at[n, what] if what < 2 else zlast.at[n],
+            src_ref=src, dst_ref=dst, send_sem=zs, recv_sem=zr.at[n] if what < 2 else zlast.at[n // 2],
             device_id=dev[to], device_id_type=MESH,
         )
 
+    def z_place(n):
+        dx, k = Z_PAIRS[n // 2]
+        return dx, (x + dx + 4) % 4, 2 * k + n % 2
+
     def z_refs(n, what):
-        dx, k = Z_STEPS[n]
-        g = (x + dx + 4) % 4
+        _, g, kk = z_place(n)
+        row = kk * SR
         if what == 0:
             return sbuf.at[n, 1, pl.ds(0, HR), :], relay.at[n, 0], "z+"
         if what == 1:
             return sbuf.at[n, 1, pl.ds(HR, HR), :], relay.at[n, 1], "z-"
         if what == 2:
-            return sbuf.at[n, 0], out.at[z, g, pl.ds(k * PR, PR), :], "z+"
+            return sbuf.at[n, 0], out.at[z, g, pl.ds(row, SR), :], "z+"
         if what == 3:
-            return sbuf.at[n, 2], out.at[z, g, pl.ds(k * PR, PR), :], "z-"
+            return sbuf.at[n, 2], out.at[z, g, pl.ds(row, SR), :], "z-"
         if what == 4:
-            return relay.at[n, 0], out.at[(z + 3) % 4, g, pl.ds(k * PR, HR), :], "z+"
-        return relay.at[n, 1], out.at[(z + 1) % 4, g, pl.ds(k * PR + HR, HR), :], "z-"
+            return relay.at[n, 0], out.at[(z + 3) % 4, g, pl.ds(row, HR), :], "z+"
+        return relay.at[n, 1], out.at[(z + 1) % 4, g, pl.ds(row + HR, HR), :], "z-"
 
     def z_send(n, what):
         src, dst, to = z_refs(n, what)
         z_copy(n, what, src, dst, to).start()
 
-    def z_wait(n, what):
-        src, dst, to = z_refs(n, what)
-        copy = z_copy(n, what, src, dst, to)
-        copy.wait_recv()
-
     def sum_step(n):
-        dx, k = Z_STEPS[n]
+        dx, k = Z_PAIRS[n]
         g = (x + dx + 4) % 4
-        copy = z_copy(n, 2, sbuf.at[n], out.at[pl.ds(0, 3), g, pl.ds(k * PR, PR), :], "z+")
+        theirs = out.at[pl.ds(0, 3), g, pl.ds(k * PR, PR), :]
+        copy = z_copy(2 * n, 2, theirs, theirs, "z+")
         copy.wait_recv()
         place = []
         for c in range(4):
@@ -255,30 +271,39 @@
         lax.fori_loop(0, PR // depth, body, 0)
 
     def hand_on(n):
-        for what in (0, 1):
-            z_wait(n, what)
-            z_send(n, what + 4)
+        copy = z_copy(n, 0, relay.at[n], relay.at[n], "z+")
+        copy.wait_recv()
+        for what in (4, 5):
+            z_send(n, what)
 
     def z_step(n):
-        dx, k = Z_STEPS[n]
+        dx, g, kk = z_place(n)
         slot = V_SLOT[dx]
-        g = (x + dx + 4) % 4
-        core_recv("X", dx, 0, k)
-        core_recv("X", dx, 1, k)
-
-        def body(r, carry):
-            acc = jnp.dot(
-                xbuf[g * 4 + r, pl.ds(k * PR, PR), :], vbuf[slot, r], preferred_element_type=jnp.float32
-            )
-            stage[r] = acc.astype(BF)
-            return carry
-
-        lax.fori_loop(0, 4, body, 0, unroll=2)
+
+        def tiles_of(gc):
+            for gy in range(2):
+                r = 2 * gy + gc
+                acc = jnp.dot(
+                    xbuf[g * 4 + r, pl.ds(kk * SR, SR), :], vbuf[slot, r], preferred_element_type=jnp.float32
+                )
+                stage[r] = acc.astype(BF)
+
+        tiles_of(core)
+        if dx == 0:
+            if kk == 0:
+                core_recv("X", 0, 0, ALL)
+        elif kk % 2 == 0:
+            core_recv("X", dx, 0, kk // 2)
+        if dx != 2 or kk // 2 in (1, 3):
+            core_recv("X", dx, 1, 10 + kk)
+        elif kk % 2 == 0:
+            core_recv("X", dx, 1, kk // 2)
+        tiles_of(1 - core)
         for rel in (2, 1, 3):
             sbuf[n, rel - 1] = stage[(z + rel - shift + 4) % 4]
         for what in (0, 1, 2, 3):
             z_send(n, what)
-        out[z, g, pl.ds(k * PR, PR), :] = stage[(z - shift + 4) % 4]
+        out[z, g, pl.ds(kk * SR, SR), :] = stage[(z - shift + 4) % 4]
 
     def relay_of(n):
         if n >= 0:
@@ -310,23 +335,28 @@
                 core_recv("Y", d, 0, k)
                 make_v(d, 0, k)
     for k in range(CH):
-        recv("y", "X", 0, 1, k)
+        recv("y", "X", 0, 1, 10 + 2 * k)
+        z_step(2 * k)
+        relay_of(2 * k - 1)
+        if k == 0:
+            for d in (1, -1):
+                core_recv("Y", d, 0, 3)
+                make_v(d, 0, 3)
+        recv("y", "X", 0, 1, 11 + 2 * k)
         if k == 2:
             recv("-", "X", 1, 0, 0)
-            send("y", "X", 1, 0, 0)
+            for h in halves_of(0):
+                send("y", "X", 1, 0, h)
         else:
             recv("-", "Y", 1, 1, min(k, 2))
         if k == 3:
             recv("+", "X", -1, 0, 0)
-            send("y", "X", -1, 0, 0)
+            for h in halves_of(0):
+                send("y", "X", -1, 0, h)
         else:
             recv("+", "Y", -1, 1, k)
-        z_step(k)
-        relay_of(k - 1)
-        if k == 0:
-            for d in (1, -1):
-                core_recv("Y", d, 0, 3)
-                make_v(d, 0, 3)
+        z_step(2 * k + 1)
+        relay_of(2 * k)
         if k < 3:
             core_recv("Y", -1, 1, k)
             make_v(-1, 1, k)
@@ -334,27 +364,53 @@
             core_recv("Y", 1, 1, min(k, 2))
             make_v(1, 1, min(k, 2))
     for u in range(8, 19):
+        pair = u - 4
+        d, k = Z_PAIRS[pair]
+        if u < 18:
+            if u == 8:
+                recv("-", "Y", 1, 1, 3)
+            if u == 16:
+                recv("+", "Y", 2, 1, 1)
+                recv("-", "Y", 2, 1, 3)
+            recv("y", "X", d, 1, 10 + 2 * k)
+            if u == 8:
+                core_recv("Y", 1, 1, 3)
+                make_v(1, 1, 3)
+            if u == 9:
+                recv("+", "Y", -1, 1, 3)
+                core_recv("Y", -1, 1, 3)
+                make_v(-1, 1, 3)
+            if u == 16:
+                for j in (1, 3):
+                    core_recv("Y", 2, 1, j)
+                    make_v(2, 1, j)
+            z_step(2 * pair)
+            relay_of(2 * pair - 1)
+        if u < 18:
+            recv("y", "X", d, 1, 11 + 2 * k)
         if u == 8:
-            recv("-", "Y", 1, 1, 3)
             recv("+", "X", -1, 0, 1)
-            send("y", "X", -1, 0, 1)
-            for d, sign, a, b in ((-1, "+", 0, 1), (1, "-", 2, 3)):
-                send(sign, "Y", d, 0, a)
-                send(sign, "Y", d, 0, b)
+            for h in halves_of(1):
+                send("y", "X", -1, 0, h)
+            for e, sign, a, b in ((-1, "+", 0, 1), (1, "-", 2, 3)):
+                send(sign, "Y", e, 0, a)
+                send(sign, "Y", e, 0, b)
             send("+", "X", -1, 0, 1)
             send("+", "Y", -1, 1, 0)
         elif u <= 11:
-            k = u - 8
-            recv("-", "X", 1, 0, k)
-            send("y", "X", 1, 0, k)
-            if k == 1:
-                recv("+", "Y", -1, 1, 3)
+            j = u - 8
+            recv("-", "X", 1, 0, j)
+            for h in halves_of(j):
+                send("y", "X", 1, 0, h)
+            if j == 1:
                 send("+", "Y", -1, 1, 1)
                 send("+", "X", -1, 0, 0)
+                send("+", "X", -1, 1, 0)
             else:
-                recv("+", "X", -1, 0, k)
-                send("y", "X", -1, 0, k)
-            if k == 3:
+                recv("+", "X", -1, 0, j)
+                for h in halves_of(j):
+                    send("y", "X", -1, 0, h)
+            if j == 3:
                 send("-", "X", 1, 0, 3)
                 send("-", "Y", 1, 1, 2)
                 send("-", "Y", 1, 1, 3)
@@ -364,56 +420,41 @@
             recv("-", "Y", 2, 0, u - 10)
         elif u == 14:
             recv("+", "X", 2, 0, 1)
-            send("y", "X", 2, 0, 1)
+            for h in halves_of(1):
+                send("y", "X", 2, 0, h)
             recv("-", "X", 2, 0, 3)
-            send("y", "X", 2, 0, 3)
-        elif u <= 16:
-            recv("+", "Y", 2, 1, u - 15)
-            recv("-", "Y", 2, 1, u - 13)
+            for h in halves_of(3):
+                send("y", "X", 2, 0, h)
+        elif u == 15:
+            recv("+", "Y", 2, 1, 0)
+            recv("-", "Y", 2, 1, 2)
         elif u == 17:
             recv("+", "X", 2, 0, 0)
             recv("-", "X", 2, 0, 2)
-        else:
+        elif u == 18:
             recv("+", "X", 2, 1, 0)
             recv("-", "X", 2, 1, 2)
-        if u < 16:
-            d, k = Z_STEPS[u - 4]
-            recv("y", "X", d, 1, k)
-            if (d, k) == (-1, 0):
-                send("+", "X", -1, 1, 0)
-            if (d, k) == (1, 2):
-                send("-", "X", 1, 1, 2)
-        elif u < 18:
-            recv("y", "X", 2, 1, 1 if u == 16 else 3)
-        if u == 8:
-            core_recv("Y", 1, 1, 3)
-            make_v(1, 1, 3)
-        if u == 9:
-            core_recv("Y", -1, 1, 3)
-            make_v(-1, 1, 3)
-        if u == 16:
-            for k in (1, 3):
-                core_recv("Y", 2, 1, k)
-                make_v(2, 1, k)
-        z_step(u - 4)
+        if (d, k) == (1, 2):
+            send("-", "X", 1, 1, 2)
         if u < 18:
-            relay_of(u - 5)
-            sum_step(u - 8)
+            z_step(2 * pair + 1)
+            relay_of(2 * pair)
+            sum_step(pair - 4)
         if u in (12, 13):
-            for k in (0, 2) if u == 12 else (1, 3):
-                core_recv("Y", 2, 0, k)
-                make_v(2, 0, k)
+            for j in (0, 2) if u == 12 else (1, 3):
+                core_recv("Y", 2, 0, j)
+                make_v(2, 0, j)
         if u == 15:
-            for k in (0, 2):
-                core_recv("Y", 2, 1, k)
-                make_v(2, 1, k)
-    z_step(4 * CH - 1)
-    for n in (13, 14, 15):
-        hand_on(n)
-        sum_step(n - 3)
-    for n in (13, 14, 15):
+            for j in (0, 2):
+                core_recv("Y", 2, 1, j)
+                make_v(2, 1, j)
+    for n in range(28, 32):
+        z_step(n)
+        relay_of(n - 1)
+    hand_on(31)
+    for n in range(10, 16):
         sum_step(n)
-    copy_of(xbuf.at[pl.ds(0, len(LINK_OPS) // CH)], ls, lr.at[0], "y").wait_send()
+    copy_of(xbuf.at[pl.ds(0, 14)], ls, lr.at[0], "y").wait_send()
     copy_of(xbuf, cs, cr.at[0], "c").wait_send()
     copy_of(out, zs, zlast.at[0], "z+").wait_send()
 
@@ -421,7 +462,7 @@
 def main_call(xin, yin, pin, qin, lrank, urank, halves, shifts):
     hbm = pl.BlockSpec(memory_space=pl.ANY)
     smem = pl.BlockSpec(memory_space=pltpu.SMEM)
-    steps = 4 * CH
+    steps = 8 * CH
     return pl.pallas_call(
         main_kernel,
         out_shape=pltpu.VMEM((4, 4, B, B), BF),
@@ -433,8 +474,8 @@
             pltpu.VMEM((3, 4, K, B), BF),
             pltpu.VMEM((B, K), BF),
             pltpu.VMEM((K, B), BF),
-            pltpu.VMEM((4, PR, B), BF),
-            pltpu.VMEM((steps, 3, PR, B), BF),
+            pltpu.VMEM((4, SR, B), BF),
+            pltpu.VMEM((steps, 3, SR, B), BF),
             pltpu.VMEM((steps, 2, HR, B), BF),
             pltpu.SemaphoreType.DMA((2 * CH + 2,)),
             pltpu.SemaphoreType.DMA,
@@ -442,8 +483,8 @@
             pltpu.SemaphoreType.DMA,
             pltpu.SemaphoreType.DMA((len(CORE_OPS),)),
             pltpu.SemaphoreType.DMA,
-            pltpu.SemaphoreType.DMA((steps, 2)),
             pltpu.SemaphoreType.DMA((steps,)),
+            pltpu.SemaphoreType.DMA((steps // 2,)),
         ],
         compiler_params=pltpu.CompilerParams(
             collective_id=0, has_side_effects=True, vmem_limit_bytes=58_000_000

time: 140 us -> 145 us (1.036)
  Pallas kernels: 137 us -> 142 us
    pallas_call x1, Pallas kernels: 137 us -> 142 us  [main_call(): pl.pallas_call(main_kernel, out_shape=pltpu.VMEM((4, 4, B, B), BF), in_sp...]
where the time goes in v4:
time: 145 us
  Pallas kernels  142 us (98%)
  local copies, waits for them, and re-layouts  3.4 us (2%)
    pallas_call x1, Pallas kernels, main_call(): pl.pallas_call(main_kernel, out_shape=pltpu.VMEM((4, 4, B, B), BF), in_sp...  142 us
    unnamed x1, local copies, waits for them, and re-layouts  3.4 us

profile of v4, /device:TPU:1, one launch (start us, length us, event | category | flops | bytes accessed | tf_op | source)
XLA Modules:
  0.0 145.3 jit_solution(16539858122647926780)
XLA Ops:
  0.0 141.9 %gather_update_exchange.1 = bf16[4,4,512,512]{3,2,1,0:T(8,128)(2,1)S(1)} custom-call(s32[32]{0:T(128)} %bitcast.12, s32[32]{0:T(128)} %bitcast.13, s32[8,16]{1,0:T(8,128)} %halves.1, s32[2,32]{1,0:T(2,128)} %shifts.1, bf16[512,1024]{1,0:T(8,128)(2,1)} %bitcast.8, bf16[512,1024]{1,0:T(8,128)(2,1)} %bitcast.9, bf16[512,1024]{1,0:T(8,128)(2,1)} %bitcast.10, ...), custom_call_target="tpu_custom_call" | custom-call | tf_op jit(solution)/shard_map/gather_update_exchange/pallas_call | solution.py:466
  141.9 3.4 %copy.10 = bf16[1,1,8192,512]{3,2,1,0:T(8,128)(2,1)} copy(bf16[1,1,8192,512]{3,2,1,0:T(8,128)(2,1)S(1)} %bitcast.7) | data formatting | bytes 16777216

commit v5 on v0

v5 whole, which is shorter than its diff:
```python
import functools

import jax
import jax.numpy as jnp
from jax import lax
from jax.experimental import pallas as pl
from jax.experimental.pallas import tpu as pltpu
from jax.sharding import PartitionSpec as P

MESH = pl.DeviceIdType.MESH
B = 512
R = 32
KP = 32
K = 1024
CH = 4
PR = B // CH
PK = K // CH
BF = jnp.bfloat16
F32 = jnp.float32


def piece_rows(k):
    return (k * PR, PR)


FULL = (0, B)
HALVES = [(i * PR // 2, PR // 2) for i in range(2 * CH)]

Y_OPS = (
    [("Y", 0, 0, k) for k in range(CH)]
    + [("X", 0, 0, h) for h in HALVES]
    + [("X", d, 0, piece_rows(k)) for k in range(1, CH) for d in (1, -1)]
)


def x_ops(sign):
    a, b = (0, 1) if sign > 0 else (2, 3)
    return (
        [("P", 0, 0, q) for q in range(CH)]
        + [("P", -sign, 0, a), ("P", -sign, 0, b)]
        + [("X", 0, 0, piece_rows(k)) for k in range(CH)]
        + [("X", 0, 1, piece_rows(0))]
        + [("X", -sign, dy, piece_rows(k)) for dy in (0, 1) for k in (a, b)]
        + [("M", sign, 0, 0), ("M", 2, 0, 0), ("M", 2, 0, 1)]
    )


LINK_OPS = [("y",) + op for op in Y_OPS] + [("+",) + op for op in x_ops(1)] + [("-",) + op for op in x_ops(-1)]
LINK_ID = {op: i for i, op in enumerate(LINK_OPS)}
CORE_OPS = (
    [("Y", 0, dy, k) for dy in (0, 1) for k in range(CH)]
    + [("X", 0, 0, FULL)]
    + [("X", 0, 1, h) for h in HALVES]
    + [("X", dx, dy, piece_rows(k)) for dx in (1, -1, 2) for dy in (0, 1) for k in range(CH)]
)
CORE_ID = {op: i for i, op in enumerate(CORE_OPS)}
Z_STEPS = (
    [(0, h) for h in HALVES]
    + [(d, piece_rows(k)) for k in range(CH) for d in (1, -1)]
    + [(2, piece_rows(k)) for k in (0, 2, 1, 3)]
)
SUMS = [(0, k) for k in range(CH)] + [(dx, row // PR) for dx, (row, _) in Z_STEPS[2 * CH :]]
Z_AT = [sum(rows for _, (_, rows) in Z_STEPS[:n]) for n in range(len(Z_STEPS))]
SLOT = {0: 0, 1: 1, -1: 2, 2: 3}


def main_kernel(
    lrank, urank, halves, shifts, xin, yin, pin, qin, out,
    xbuf, ybuf, vbuf, pbuf, mout, minto, mrel, qtbuf, stage, sbuf, relay,
    in_sem, ls, lr, cs, cr, zs, zr, zlast,
):
    front, tile = lax.axis_index("front"), lax.axis_index("tile")
    yh, z = front // 4, front % 4
    x, yl, core = tile // 4, (tile // 2) % 2, tile % 2

    def tile_at(gx, gy, gc):
        return (gx * 2 + gy) * 2 + gc

    dev = {
        "y": (front, tile_at(x, 1 - yl, core)),
        "+": (front, tile_at((x + 1) % 4, yl, core)),
        "-": (front, tile_at((x + 3) % 4, yl, core)),
        "c": (front, tile_at(x, yl, 1 - core)),
        "z+": (yh * 4 + (z + 1) % 4, tile),
        "z-": (yh * 4 + (z + 3) % 4, tile),
    }

    def row_of(dx, dy, gc):
        gy = yl if dy == 0 else 1 - yl
        return tile_at((x + dx + 4) % 4, gy, gc)

    def piece(kind, dx, dy, gc, k):
        if kind == "X":
            return xbuf.at[row_of(dx, dy, gc), pl.ds(*k), :]
        gy = yl if dy == 0 else 1 - yl
        return ybuf.at[2 * gy + gc, pl.ds(k * PK, PK), :]

    def copy_of(src, dst, ssem, rsem, to):
        return pltpu.make_async_remote_copy(
            src_ref=src, dst_ref=dst, send_sem=ssem, recv_sem=rsem,
            device_id=dev[to], device_id_type=MESH,
        )

    def send(link, kind, dx, dy, k):
        i = LINK_ID[(link, kind, dx, dy, k)]
        sign = 1 if link == "+" else -1
        if kind == "P":
            src = pbuf.at[SLOT[dx], k]
            dst = pbuf.at[SLOT[-sign] if dx == 0 else SLOT[2], k]
        elif kind == "M":
            part = pl.ds(0 if sign > 0 else 2, 2)
            if dx == sign:
                src, dst = mout.at[SLOT[sign] - 1], minto.at[SLOT[-sign] - 1]
            elif k == 0:
                src, dst = mout.at[SLOT[2] - 1, part], mrel.at[0 if sign > 0 else 1]
            else:
                src, dst = mrel.at[0 if sign > 0 else 1], minto.at[SLOT[2] - 1, part]
        else:
            src = dst = piece(kind, dx, dy, core, k)
        copy_of(src, dst, ls, lr.at[i], link).start()

    def core_send(kind, dx, dy, k):
        i = CORE_ID[(kind, dx, dy, k)]
        ref = piece(kind, dx, dy, core, k)
        copy_of(ref, ref, cs, cr.at[i], "c").start()

    def core_recv(kind, dx, dy, k):
        i = CORE_ID[(kind, dx, dy, k)]
        ref = piece(kind, dx, dy, 1 - core, k)
        copy = copy_of(ref, ref, cs, cr.at[i], "c")
        copy.wait_recv()

    def await_link(link, sender, ref):
        copy = copy_of(ref, ref, ls, lr.at[LINK_ID[(link,) + sender]], link)
        copy.wait_recv()

    def recv(link, kind, dx, dy, k):
        if link == "y":
            sender = (kind, dx, 1 - dy, k)
        elif link == "+":
            sender = (kind, (dx + 2) % 4 - 1, dy, k)
        else:
            sender = (kind, dx % 4 - 1, dy, k)
        await_link(link, sender, piece(kind, dx, dy, core, k))
        core_send(kind, dx, dy, k)

    def recv_p(dx, q):
        if dx == 2:
            sign = 1 if q < 2 else -1
            sender = ("P", -sign, 0, q)
        else:
            sign = -dx
            sender = ("P", 0, 0, q)
        await_link("+" if sign > 0 else "-", sender, pbuf.at[SLOT[dx], q])

    me = tile

    def raw(n, k):
        return vbuf.at[3, n, pl.ds(k // 2 * B, B), pl.ds(k % 2 * PK, PK)]

    def columns(ref, k):
        return ref.at[:, pl.ds(k * PK, PK)]

    y_loads, p_loads, q_loads = [], [], []
    for k in range(CH):
        y_loads.append(pltpu.make_async_copy(columns(yin, k), raw(0, k), in_sem.at[k]))
        p_loads.append(pltpu.make_async_copy(columns(pin, k), pbuf.at[0, k], in_sem.at[CH + k]))
        q_loads.append(pltpu.make_async_copy(columns(qin, k), raw(1, k), in_sem.at[2 * CH + k]))
    x_load = pltpu.make_async_copy(xin, xbuf.at[me], in_sem.at[3 * CH])
    for copy in y_loads + p_loads + [x_load] + q_loads:
        copy.start()

    barrier = pltpu.get_barrier_semaphore()
    for name in ("y", "+", "-", "c", "z+", "z-"):
        pl.semaphore_signal(barrier, inc=1, device_id=dev[name], device_id_type=MESH)

    col = lax.broadcasted_iota(jnp.int32, (8, K), 1)

    def keep(ranks):
        limit = jnp.zeros((8, K), jnp.int32)
        for k in range(KP):
            limit = jnp.where(col // R == k, ranks[k], limit)
        return (col % R < limit).astype(F32)[:1]

    lkeep = keep(lrank)
    ukeep = keep(urank)

    def ready(k):
        cols = slice(k * PK, (k + 1) * PK)
        y_loads[k].wait()
        part = raw(0, k)[...].astype(F32) * lkeep[:, cols]
        ybuf[2 * yl + core, cols, :] = part.T.astype(BF)
        p_loads[k].wait()
        pbuf[0, k] = (pbuf[0, k].astype(F32) * ukeep[:, cols]).astype(BF)

    ready(0)
    pl.semaphore_wait(barrier, 6)
    for k in range(CH):
        if k + 1 < CH:
            ready(k + 1)
        send("y", "Y", 0, 0, k)
        core_send("Y", 0, 0, k)
        send("+", "P", 0, 0, k)
        send("-", "P", 0, 0, k)
    x_load.wait()
    for h in HALVES:
        send("y", "X", 0, 0, h)
    core_send("X", 0, 0, FULL)
    for k in range(CH):
        q_loads[k].wait()
        qtbuf[k * PK : (k + 1) * PK, :] = raw(1, k)[...].astype(F32).T.astype(BF)

    def same_panel():
        a = lax.broadcasted_iota(jnp.int32, (PK, PK), 0) // R
        return a == lax.broadcasted_iota(jnp.int32, (PK, PK), 1) // R

    def middle(r, slot, q):
        rows = slice(q * PK, (q + 1) * PK)
        m = jnp.dot(ybuf[r, rows, :], pbuf[slot, q], preferred_element_type=F32)
        return jnp.where(same_panel(), m, 0.0)

    def put_v(slot, rs, q, middles):
        rows = slice(q * PK, (q + 1) * PK)
        for r, m in zip(rs, middles):
            v = jnp.dot(m, qtbuf[rows, :], preferred_element_type=F32)
            vbuf[slot, r, rows, :] = v.astype(BF)

    def own_v(dy, k, classes=(0, 1)):
        gy = yl if dy == 0 else 1 - yl
        rs = [2 * gy + (core if c == 0 else 1 - core) for c in classes]
        put_v(0, rs, k, [middle(r, 0, k).astype(BF) for r in rs])

    def make_m(dx, q):
        for r in range(4):
            m = middle(r, SLOT[dx], q)
            m = m[:, : PK // 2] + m[:, PK // 2 :]
            for t in range(2):
                part = [m[t * 128 + i * R : t * 128 + (i + 1) * R] for i in range(4)]
                mout[SLOT[dx] - 1, q, r, t * R : (t + 1) * R, :] = (part[0] + part[1] + part[2] + part[3]).astype(BF)

    def far_v(dx, q):
        middles = []
        for r in range(4):
            m = minto[SLOT[dx] - 1, q, r].astype(F32)
            m = jnp.concatenate([m[:R]] * 4 + [m[R:]] * 4, axis=0)
            m = jnp.concatenate([m, m], axis=1)
            middles.append(jnp.where(same_panel(), m, 0.0).astype(BF))
        put_v(SLOT[dx], range(4), q, middles)

    col_half = [halves[4 * yh + c, tile] for c in range(4)]
    col_shift = [shifts[yh, tile + 16 * col_half[c]] for c in range(4)]
    half = halves[front, tile]
    shift = shifts[yh, tile + 16 * half]

    def sum_of(n):
        dx, (row, _) = Z_STEPS[n]
        return SUMS.index((dx, row // PR))

    def z_copy(n, what, src, dst, to):
        rsem = zr.at[n] if what < 2 else zlast.at[sum_of(n)]
        return copy_of(src, dst, zs, rsem, to)

    def z_send(n, what):
        dx, (row, rows) = Z_STEPS[n]
        g = (x + dx + 4) % 4
        hr, at = rows // 2, Z_AT[n]
        passing = [relay.at[i, pl.ds(at // 2, hr), :] for i in range(2)]
        src, dst, to = [
            (sbuf.at[1, pl.ds(at, hr), :], passing[0], "z+"),
            (sbuf.at[1, pl.ds(at + hr, hr), :], passing[1], "z-"),
            (sbuf.at[0, pl.ds(at, rows), :], out.at[z, g, pl.ds(row, rows), :], "z+"),
            (sbuf.at[2, pl.ds(at, rows), :], out.at[z, g, pl.ds(row, rows), :], "z-"),
            (passing[0], out.at[(z + 3) % 4, g, pl.ds(row, hr), :], "z+"),
            (passing[1], out.at[(z + 1) % 4, g, pl.ds(row + hr, hr), :], "z-"),
        ][what]
        z_copy(n, what, src, dst, to).start()

    def hand_on(n):
        _, (_, rows) = Z_STEPS[n]
        both = relay.at[:, pl.ds(Z_AT[n] // 2, rows // 2), :]
        copy = z_copy(n, 0, both, both, "z+")
        copy.wait_recv()
        for what in (4, 5):
            z_send(n, what)

    handed = []

    def relay_upto(n):
        while len(handed) <= n:
            hand_on(len(handed))
            handed.append(n)

    def sum_step(n):
        dx, k = SUMS[n]
        g = (x + dx + 4) % 4
        theirs = out.at[pl.ds(0, 3), g, pl.ds(k * PR, PR), :]
        copy = copy_of(theirs, theirs, zs, zlast.at[n], "z+")
        copy.wait_recv()
        place = []
        for c in range(4):
            row = 4 * g + (z - col_shift[c] + 4) % 4
            place.append(2 * col_half[c] + halves[4 * yh + c, row])
        depth = 16

        def body(i, carry):
            rows = pl.ds(pl.multiple_of(k * PR + i * depth, depth), depth)
            tiles = [out[c, g, rows, :].astype(jnp.float32) for c in range(4)]
            for s in range(4):
                total = jnp.zeros((depth, B), jnp.float32)
                for c in range(4):
                    total = total + jnp.where(place[c] == s, tiles[c], 0.0)
                out[s, g, rows, :] = total.astype(BF)
            return carry

        lax.fori_loop(0, PR // depth, body, 0)

    pending = []

    def later(work, *args):
        pending.append(functools.partial(work, *args))

    def run_some(count):
        for _ in range(min(count, len(pending))):
            pending.pop(0)()

    def z_step(n):
        dx, (row, rows) = Z_STEPS[n]
        g = (x + dx + 4) % 4
        at = Z_AT[n]

        def tiles_of(gc):
            for gy in range(2):
                r = 2 * gy + gc
                acc = jnp.dot(
                    xbuf[g * 4 + r, pl.ds(row, rows), :], vbuf[SLOT[dx], r], preferred_element_type=F32
                )
                stage[r, :rows] = acc.astype(BF)

        tiles_of(core)
        run_some(1)
        if dx != 0:
            core_recv("X", dx, 0, (row, rows))
        elif n == 0:
            core_recv("X", 0, 0, FULL)
        core_recv("X", dx, 1, (row, rows))
        tiles_of(1 - core)
        for rel in (2, 1, 3):
            sbuf[rel - 1, at : at + rows, :] = stage[(z + rel - shift + 4) % 4, :rows]
        for what in (0, 1, 2, 3):
            z_send(n, what)
        out[z, g, row : row + rows, :] = stage[(z - shift + 4) % 4, :rows]

    def pass_on(link, dx, k):
        recv(link, "X", dx, 0, piece_rows(k))
        send("y", "X", dx, 0, piece_rows(k))

    both = (("-", 1), ("+", -1))

    for k in range(CH):
        own_v(0, k, (0,))
    for k in range(CH):
        core_recv("Y", 0, 0, k)
        own_v(0, k, (1,))
    for k in range(CH):
        recv("y", "Y", 0, 1, k)
        if k == 3:
            own_v(1, k, (0,))
        for dx in (1, -1):
            recv_p(dx, k)
        if k == 3:
            for link, _ in both:
                send(link, "X", 0, 0, piece_rows(0))
        core_recv("Y", 0, 1, k)
        own_v(1, k, (0, 1) if k < 3 else (1,))
        make_m(1, k)
        make_m(-1, k)
    send("+", "M", 1, 0, 0)
    send("-", "M", -1, 0, 0)
    for h in range(2 * CH):
        recv("y", "X", 0, 1, HALVES[h])
        if h == 1:
            for link, dx in both:
                send(link, "X", 0, 1, piece_rows(0))
                send(link, "X", 0, 0, piece_rows(1))
                for q, k in ((0, 2), (1, 3)) if link == "+" else ((2, 2), (3, 3)):
                    send(link, "P", dx, 0, q)
                    send(link, "X", 0, 0, piece_rows(k))
        z_step(h)
        relay_upto(h - 1)
        if h == 2:
            for link, dx in both:
                recv(link, "X", dx, 0, piece_rows(0))
        if h == 4:
            await_link("-", ("M", -1, 0, 0), minto.at[SLOT[1] - 1])
            await_link("+", ("M", 1, 0, 0), minto.at[SLOT[-1] - 1])
            for q in range(CH):
                later(far_v, 1, q)
            for q in range(CH):
                later(far_v, -1, q)
        if h == 5:
            for link, dx in both:
                recv(link, "X", dx, 1, piece_rows(0))
        if h == 7:
            for link, dx in both:
                pass_on(link, dx, 1)
        if h > 4:
            run_some(1)
    while pending:
        run_some(1)
    for n in range(8, 20):
        dx, (row, _) = Z_STEPS[n]
        if 10 <= n < 16:
            recv("y", "X", dx, 1, (row, PR))
        z_step(n)
        relay_upto(n - 1 if n < 17 else n - 2)
        if n in (8, 10):
            for q in (0, 2) if n == 8 else (1, 3):
                recv_p(2, q)
                make_m(2, q)
        if n == 10:
            send("+", "M", 2, 0, 0)
            send("-", "M", 2, 0, 0)
        if n in (9, 11):
            for link, e in both:
                pass_on(link, e, 2 if n == 9 else 3)
        if n == 10:
            for k in (0, 1):
                send("+", "X", -1, 0, piece_rows(k))
            send("-", "X", 1, 0, piece_rows(2))
        if n == 11:
            send("-", "X", 1, 0, piece_rows(3))
        if n == 12:
            for link, i in (("+", 0), ("-", 1)):
                await_link(link, ("M", 2, 0, 0), mrel.at[i])
                send(link, "M", 2, 0, 1)
            send("+", "X", -1, 1, piece_rows(0))
            send("+", "X", -1, 1, piece_rows(1))
            send("-", "X", 1, 1, piece_rows(2))
        if n == 13:
            recv("+", "X", 2, 0, piece_rows(0))
            recv("-", "X", 2, 0, piece_rows(2))
        if n == 14:
            send("-", "X", 1, 1, piece_rows(3))
            recv("+", "X", 2, 0, piece_rows(1))
            recv("-", "X", 2, 0, piece_rows(3))
        if n == 15:
            for link, i in (("+", 0), ("-", 2)):
                await_link(link, ("M", 2, 0, 1), minto.at[SLOT[2] - 1, pl.ds(i, 2)])
            for q in range(CH):
                far_v(2, q)
            recv("+", "X", 2, 1, piece_rows(0))
            recv("-", "X", 2, 1, piece_rows(2))
        if n == 17:
            recv("+", "X", 2, 1, piece_rows(1))
            recv("-", "X", 2, 1, piece_rows(3))
        if 10 <= n < 18:
            later(sum_step, n - 10)
    while pending:
        run_some(1)
    for n in (18, 19):
        relay_upto(n)
    for n in range(8, 16):
        sum_step(n)
    twelve, ten = xbuf.at[pl.ds(0, 12)], xbuf.at[pl.ds(0, 10)]
    copy_of(twelve, twelve, ls, lr.at[0], "y").wait_send()
    copy_of(ten, ten, cs, cr.at[0], "c").wait_send()
    copy_of(out, out, zs, zlast.at[0], "z+").wait_send()


def main_call(xin, yin, pin, qin, lrank, urank, halves, shifts):
    hbm = pl.BlockSpec(memory_space=pl.ANY)
    smem = pl.BlockSpec(memory_space=pltpu.SMEM)
    return pl.pallas_call(
        main_kernel,
        out_shape=pltpu.VMEM((4, 4, B, B), BF),
        in_specs=[smem] * 4 + [hbm] * 4,
        out_specs=pl.BlockSpec(memory_space=pltpu.VMEM),
        scratch_shapes=[
            pltpu.VMEM((16, B, K), BF),
            pltpu.VMEM((4, K, B), BF),
            pltpu.VMEM((4, 4, K, B), BF),
            pltpu.VMEM((4, CH, B, PK), BF),
            pltpu.VMEM((3, CH, 4, 2 * R, 128), BF),
            pltpu.VMEM((3, CH, 4, 2 * R, 128), BF),
            pltpu.VMEM((2, 2, 4, 2 * R, 128), BF),
            pltpu.VMEM((K, B), BF),
            pltpu.VMEM((4, PR, B), BF),
            pltpu.VMEM((3, 4 * B, B), BF),
            pltpu.VMEM((2, 2 * B, B), BF),
            pltpu.SemaphoreType.DMA((3 * CH + 1,)),
            pltpu.SemaphoreType.DMA,
            pltpu.SemaphoreType.DMA((len(LINK_OPS),)),
            pltpu.SemaphoreType.DMA,
            pltpu.SemaphoreType.DMA((len(CORE_OPS),)),
            pltpu.SemaphoreType.DMA,
            pltpu.SemaphoreType.DMA((len(Z_STEPS),)),
            pltpu.SemaphoreType.DMA((len(SUMS),)),
        ],
        compiler_params=pltpu.CompilerParams(
            collective_id=0, has_side_effects=True, vmem_limit_bytes=58_000_000
        ),
        name="gather_update_exchange",
    )(lrank, urank, halves, shifts, xin, yin, pin, qin)


def per_device(lower_basis, lower_coeff, upper_basis, upper_coeff, lower_rank, upper_rank, child_half, owner_shift):
    blocks = main_call(
        lower_basis[0, 0], lower_coeff[0, 0], upper_basis[0, 0], upper_coeff[0, 0],
        lower_rank[0, 0], upper_rank[0, 0], child_half, owner_shift,
    )
    return blocks.reshape(1, 1, 16 * B, B)


def solution(mesh):
    whole = P("front", "tile", None, None)
    ranks = P("front", "tile", None)
    return jax.shard_map(
        per_device,
        mesh=mesh,
        in_specs=(whole, whole, whole, whole, ranks, ranks, P(), P()),
        out_specs=whole,
        check_vma=False,
    )
```

time: 500 us -> 138 us (0.28)
  waiting for transfers between devices: 303 us -> 0 us
  Pallas kernels: 0 us -> 134 us
  matrix products: 83.4 us -> 0 us
  local copies, waits for them, and re-layouts: 66.3 us -> 3.4 us
  between operations: 26.3 us -> 0.01 us
  other arithmetic: 14.5 us -> 0 us
    all_gather x2 -> x0, waiting for transfers between devices: 155 us -> none  [the longest x1 83.4 us: per_device(): coeffs = lax.all_gather(lower_coeff[0], 'tile', axis=0, tiled=True)]
    ppermute x2 -> x0, waiting for transfers between devices: 147 us -> none  [partner(): return lax.ppermute(block, axis, route)]
    pallas_call x0 -> x1, Pallas kernels: none -> 134 us  [main_call(): pl.pallas_call(main_kernel, out_shape=pltpu.VMEM((4, 4, B, B), BF), in_sp...]
    dot_general x6 -> x0, matrix products: 83.4 us -> none  [the longest x4 46.9 us: per_device(): jnp.dot(one_hot, one_block, preferred_element_type=jnp.float32)]
    all_gather x2 -> x0, local copies, waits for them, and re-layouts: 43.6 us -> none  [the longest x1 22 us: per_device(): coeffs = lax.all_gather(lower_coeff[0], 'tile', axis=0, tiled=True)]
    unnamed x19 -> x1, local copies, waits for them, and re-layouts: 12.3 us -> 3.4 us
    reshape x5 -> x0, local copies, waits for them, and re-layouts: 8.32 us -> none  [the longest x1 8 us: per_device(): return assembled.astype(jnp.bfloat16).reshape(1, 1, tile_count * B, B)]
    squeeze x1 -> x0, other arithmetic: 5.89 us -> none  [per_device(): lax.dynamic_index_in_dim(holding, (my_child ^ 1) % 2, 2, keepdims=False)]
  transfers between devices with their start and end apart: 4 -> 0, of which waited for: 4 -> 0; matrix products, arithmetic and copies ran while one was open for 11% -> 0% of each run, Pallas kernels for 0% -> 0%
where the time goes in v5:
time: 138 us
  Pallas kernels  134 us (97%)
  local copies, waits for them, and re-layouts  3.4 us (2%)
    pallas_call x1, Pallas kernels, main_call(): pl.pallas_call(main_kernel, out_shape=pltpu.VMEM((4, 4, B, B), BF), in_sp...  134 us
    unnamed x1, local copies, waits for them, and re-layouts  3.4 us

profile of v5, /device:TPU:1, one launch (start us, length us, event | category | flops | bytes accessed | tf_op | source)
XLA Modules:
  0.0 137.6 jit_solution(13176903695182591683)
XLA Ops:
  0.0 134.2 %gather_update_exchange.1 = bf16[4,4,512,512]{3,2,1,0:T(8,128)(2,1)S(1)} custom-call(s32[32]{0:T(128)} %bitcast.12, s32[32]{0:T(128)} %bitcast.13, s32[8,16]{1,0:T(8,128)} %halves.1, s32[2,32]{1,0:T(2,128)} %shifts.1, bf16[512,1024]{1,0:T(8,128)(2,1)} %bitcast.8, bf16[512,1024]{1,0:T(8,128)(2,1)} %bitcast.9, bf16[512,1024]{1,0:T(8,128)(2,1)} %bitcast.10, ...), custom_call_target="tpu_custom_call" | custom-call | tf_op jit(solution)/shard_map/gather_update_exchange/pallas_call | solution.py:473
  134.2 3.4 %copy.10 = bf16[1,1,8192,512]{3,2,1,0:T(8,128)(2,1)} copy(bf16[1,1,8192,512]{3,2,1,0:T(8,128)(2,1)S(1)} %bitcast.7) | data formatting | bytes 16777216

commit v6 on v5

--- a/solution.py
+++ b/solution.py
@@ -183,25 +183,38 @@
         return (col % R < limit).astype(F32)[:1]
 
     lkeep = keep(lrank)
-    ukeep = keep(urank)
-
-    def ready(k):
-        cols = slice(k * PK, (k + 1) * PK)
+
+    def turn_y(k):
         y_loads[k].wait()
-        part = raw(0, k)[...].astype(F32) * lkeep[:, cols]
-        ybuf[2 * yl + core, cols, :] = part.T.astype(BF)
-        p_loads[k].wait()
-        pbuf[0, k] = (pbuf[0, k].astype(F32) * ukeep[:, cols]).astype(BF)
-
-    ready(0)
-    pl.semaphore_wait(barrier, 6)
-    for k in range(CH):
-        if k + 1 < CH:
-            ready(k + 1)
+        part = raw(0, k)[...].astype(F32) * lkeep[:, k * PK : (k + 1) * PK]
+        ybuf[2 * yl + core, k * PK : (k + 1) * PK, :] = part.T.astype(BF)
+
+    def send_y(k):
         send("y", "Y", 0, 0, k)
         core_send("Y", 0, 0, k)
+
+    turn_y(0)
+    pl.semaphore_wait(barrier, 6)
+    send_y(0)
+    ukeep = keep(urank)
+
+    def mask_p(k):
+        p_loads[k].wait()
+        pbuf[0, k] = (pbuf[0, k].astype(F32) * ukeep[:, k * PK : (k + 1) * PK]).astype(BF)
+
+    def send_p(k):
         send("+", "P", 0, 0, k)
         send("-", "P", 0, 0, k)
+
+    mask_p(0)
+    turn_y(1)
+    send_p(0)
+    for k in range(1, CH):
+        mask_p(k)
+        if k + 1 < CH:
+            turn_y(k + 1)
+        send_y(k)
+        send_p(k)
     x_load.wait()
     for h in HALVES:
         send("y", "X", 0, 0, h)
@@ -405,10 +418,10 @@
                 pass_on(link, dx, 1)
         if h > 4:
             run_some(1)
-    while pending:
-        run_some(1)
     for n in range(8, 20):
         dx, (row, _) = Z_STEPS[n]
+        if n == 9:
+            run_some(len(pending))
         if 10 <= n < 16:
             recv("y", "X", dx, 1, (row, PR))
         z_step(n)

time: 138 us -> 137 us (level)
  no operation moved by 1% of the time
where the time goes in v6:
time: 137 us
  Pallas kernels  134 us (98%)
  local copies, waits for them, and re-layouts  3.4 us (2%)
    pallas_call x1, Pallas kernels, main_call(): pl.pallas_call(main_kernel, out_shape=pltpu.VMEM((4, 4, B, B), BF), in_sp...  134 us
    unnamed x1, local copies, waits for them, and re-layouts  3.4 us

profile of v6, /device:TPU:1, one launch (start us, length us, event | category | flops | bytes accessed | tf_op | source)
XLA Modules:
  0.0 137.2 jit_solution(11223247188987180998)
XLA Ops:
  0.0 133.8 %gather_update_exchange.1 = bf16[4,4,512,512]{3,2,1,0:T(8,128)(2,1)S(1)} custom-call(s32[32]{0:T(128)} %bitcast.12, s32[32]{0:T(128)} %bitcast.13, s32[8,16]{1,0:T(8,128)} %halves.1, s32[2,32]{1,0:T(2,128)} %shifts.1, bf16[512,1024]{1,0:T(8,128)(2,1)} %bitcast.8, bf16[512,1024]{1,0:T(8,128)(2,1)} %bitcast.9, bf16[512,1024]{1,0:T(8,128)(2,1)} %bitcast.10, ...), custom_call_target="tpu_custom_call" | custom-call | tf_op jit(solution)/shard_map/gather_update_exchange/pallas_call | solution.py:486
  133.8 3.4 %copy.10 = bf16[1,1,8192,512]{3,2,1,0:T(8,128)(2,1)} copy(bf16[1,1,8192,512]{3,2,1,0:T(8,128)(2,1)S(1)} %bitcast.7) | data formatting | bytes 16777216

commit v7 on v6

--- a/solution.py
+++ b/solution.py
@@ -350,7 +350,8 @@
                 stage[r, :rows] = acc.astype(BF)
 
         tiles_of(core)
-        run_some(1)
+        if n != 8:
+            run_some(1)
         if dx != 0:
             core_recv("X", dx, 0, (row, rows))
         elif n == 0:
@@ -416,16 +417,23 @@
         if h == 7:
             for link, dx in both:
                 pass_on(link, dx, 1)
-        if h > 4:
+        if 4 < h < 7:
             run_some(1)
+
+    def second_hop():
+        for link, e in both:
+            pass_on(link, e, 2)
+
     for n in range(8, 20):
-        dx, (row, _) = Z_STEPS[n]
-        if n == 9:
+        if n == 10:
+            pending.insert(0, second_hop)
+        z_step(n)
+        if 10 <= n + 1 < 16:
+            ahead = Z_STEPS[n + 1]
+            recv("y", "X", ahead[0], 1, ahead[1])
+        relay_upto(n - 1 if n < 17 else n - 2)
+        if n == 8:
             run_some(len(pending))
-        if 10 <= n < 16:
-            recv("y", "X", dx, 1, (row, PR))
-        z_step(n)
-        relay_upto(n - 1 if n < 17 else n - 2)
         if n in (8, 10):
             for q in (0, 2) if n == 8 else (1, 3):
                 recv_p(2, q)
@@ -433,9 +441,9 @@
         if n == 10:
             send("+", "M", 2, 0, 0)
             send("-", "M", 2, 0, 0)
-        if n in (9, 11):
+        if n == 11:
             for link, e in both:
-                pass_on(link, e, 2 if n == 9 else 3)
+                pass_on(link, e, 3)
         if n == 10:
             for k in (0, 1):
                 send("+", "X", -1, 0, piece_rows(k))

time: 137 us -> 136 us (level)
  no operation moved by 1% of the time
where the time goes in v7:
time: 136 us
  Pallas kernels  133 us (98%)
  local copies, waits for them, and re-layouts  3.4 us (2%)
    pallas_call x1, Pallas kernels, main_call(): pl.pallas_call(main_kernel, out_shape=pltpu.VMEM((4, 4, B, B), BF), in_sp...  133 us
    unnamed x1, local copies, waits for them, and re-layouts  3.4 us

profile of v7, /device:TPU:1, one launch (start us, length us, event | category | flops | bytes accessed | tf_op | source)
XLA Modules:
  0.0 136.2 jit_solution(7929352690329083451)
XLA Ops:
  0.0 132.8 %gather_update_exchange.1 = bf16[4,4,512,512]{3,2,1,0:T(8,128)(2,1)S(1)} custom-call(s32[32]{0:T(128)} %bitcast.12, s32[32]{0:T(128)} %bitcast.13, s32[8,16]{1,0:T(8,128)} %halves.1, s32[2,32]{1,0:T(2,128)} %shifts.1, bf16[512,1024]{1,0:T(8,128)(2,1)} %bitcast.8, bf16[512,1024]{1,0:T(8,128)(2,1)} %bitcast.9, bf16[512,1024]{1,0:T(8,128)(2,1)} %bitcast.10, ...), custom_call_target="tpu_custom_call" | custom-call | tf_op jit(solution)/shard_map/gather_update_exchange/pallas_call | solution.py:494
  132.8 3.4 %copy.10 = bf16[1,1,8192,512]{3,2,1,0:T(8,128)(2,1)} copy(bf16[1,1,8192,512]{3,2,1,0:T(8,128)(2,1)S(1)} %bitcast.7) | data formatting | bytes 16777216
